TPU v7x, 128 devices: a whole 4x4x4 slice. The times are simulated.
128 devices in a mesh: gx: 32 (over z, x, core), gy: 4 (over y).
Axes of the slice: x: 4, y: 4, z: 4, core: 2. Of those that a mesh axis runs over, the one named last changes fastest.
Arguments:
- velocity: float32 [3, 32768, 512], P(None, ('gx', 'gy')), may hold values from -6 to 6
- positions: float32 [3, 4096, 256], P(None, ('gx', 'gy')), may hold values from -6 to 6
- stiff_h: float32 [4096, 256], P(('gx', 'gy')), may hold values from 0.1 to 1
- stiff_v: float32 [4096, 256], P(('gx', 'gy')), may hold values from 0.1 to 1
- marker_owner: int32 [1048576, 1], P(('gx', 'gy')), may hold values from 0 to 127; in each aligned block of 8192 rows (0 to 8191, 8192 to 16383, ...) at most 96 rows name the same one
- marker_element: int32 [1048576], P(('gx', 'gy')), may hold values from 0 to 255
- marker_coords: float32 [3, 1048576], P(None, ('gx', 'gy')), may hold values from -1 to 1
Outputs:
- new_positions: float32 [3, 4096, 256], P(None, ('gx', 'gy'))
- node_forces: float32 [3, 32768, 512], P(None, ('gx', 'gy'))
Inputs may be any that keep to these rules, and one draw needn't show every extreme that they name: `marker_owner`: among the markers of one device's rows, no owner is named more than 96 times, and in some devices' rows one owner is named exactly 96 times.
All inputs are finite; a program needn't handle non-finite values.
Results may differ from a plain program's by a relative error of at most 0.00013.
Values sent between devices are 32-bit elements; how exact they have to be, the bound alone decides.
A program may use at most 64 MiB of HBM per device.

v0:
```python
import math

import jax
import jax.numpy as jnp
from jax import lax
from jax.sharding import PartitionSpec as P

POINTS = 8


bend_modulus = 0.05
time_step = 0.5


def with_halo(x, sides, width):
    edges = {}
    for axis, dim in sides:
        peers, length = (lax.axis_size(axis), x.shape[dim])
        up = [(i, (i + 1) % peers) for i in range(peers)]
        last = lax.slice_in_dim(x, length - width, length, axis=dim)
        leading = lax.slice_in_dim(x, 0, width, axis=dim)
        edges[dim] = (
            lax.ppermute(last, axis, up),
            lax.ppermute(leading, axis, [(b, a) for a, b in up]),
        )
    done = []
    for _, dim in sides:
        low, high = edges[dim]
        around = [(width, width) if d in done else (0, 0) for d in range(x.ndim)]
        x = jnp.concatenate([jnp.pad(low, around), x, jnp.pad(high, around)], axis=dim)
        done.append(dim)
    return x


def split_up(x, dim, peers):
    dims = x.shape
    tiles = x.reshape(*dims[:dim], peers, dims[dim] // peers, *dims[dim + 1 :])
    return jnp.moveaxis(tiles, dim, 0)


def piece_ends(length, count):
    hop = length // count
    if hop >= 8:
        hop -= hop % 8
    return [hop * k for k in range(1, count)]


def in_order(tiles, dim):
    tiles = jnp.moveaxis(tiles, 0, dim)
    dims = tiles.shape
    return tiles.reshape(*dims[:dim], dims[dim] * dims[dim + 1], *dims[dim + 2 :])


def exchange_in_pieces(x, axis, pieces, split_dim, concat_dim):
    tiles = split_up(x, split_dim, lax.axis_size(axis))
    cut = max(range(1, max(2, tiles.ndim - 1)), key=lambda d: tiles.shape[d])
    outs = []
    for share in jnp.split(tiles, piece_ends(tiles.shape[cut], pieces), axis=cut):
        if share.size:
            outs.append(lax.all_to_all(share, axis, split_axis=0, concat_axis=0, tiled=True))
    return in_order(jnp.concatenate(outs, axis=cut), concat_dim)


def basis(values):
    abscissa = -jnp.cos(jnp.pi * jnp.arange(POINTS).astype(values.dtype) / (POINTS - 1))
    collected = []
    for i in range(POINTS):
        product = jnp.ones_like(values)
        for j in range(POINTS):
            if j != i:
                product = product * ((values - abscissa[j]) / (abscissa[i] - abscissa[j]))
        collected.append(product)
    return jnp.stack(collected)


def weight_table(factors):
    along_r = factors[0:POINTS].T
    along_s = factors[POINTS : 2 * POINTS].T
    along_t = factors[2 * POINTS : 3 * POINTS].T
    table = along_r[:, :, None, None] * along_s[:, None, :, None] * along_t[:, None, None, :]
    return table.reshape(along_r.shape[0], POINTS * POINTS * POINTS)


def surface_laplacian(extended):
    middle = extended[:, 1:-1]
    return (
        extended[:, 2:]
        + extended[:, :-2]
        + jnp.roll(middle, 1, axis=2)
        + jnp.roll(middle, -1, axis=2)
        - 4.0 * middle
    )


def tension(extended, stiff_h):
    points = extended[:3]
    vertical = extended[3]
    middle = points[:, 1:-1]
    return (
        stiff_h * (jnp.roll(middle, -1, axis=2) - middle)
        + jnp.roll(stiff_h, 1, axis=1) * (jnp.roll(middle, 1, axis=2) - middle)
        + vertical[1:-1] * (points[:, 2:] - middle)
        + vertical[:-2] * (points[:, :-2] - middle)
    )


def three_factors(coords):
    return jnp.concatenate([basis(coords[0]), basis(coords[1]), basis(coords[2])], axis=0)


def selector_of(block_elements, elem_count):
    return (block_elements[:, None] == jnp.arange(elem_count, dtype=jnp.int32)[None, :]).astype(
        jnp.float32
    )


def local(velocity, positions, stiff_h, stiff_v, marker_owner, marker_element, marker_coords):
    major_count = lax.axis_size("gx")
    minor_count = lax.axis_size("gy")
    devices_all = major_count * minor_count
    marker_count = marker_owner.shape[0]
    capacity = 3 * marker_count // (2 * devices_all)
    slot_total = devices_all * capacity
    elem_count = velocity.shape[1]
    stacked = jnp.concatenate([positions, stiff_v[None]], axis=0)
    extended = with_halo(stacked, ((("gx", "gy"), 1),), 2)
    pulling = tension(extended[:, 1:-1], stiff_h)
    laplace = surface_laplacian(extended[:3])
    bending = -bend_modulus * surface_laplacian(laplace)
    marker_force = (pulling + bending).reshape(3, marker_count)
    owners = marker_owner[:, 0]
    ordering = jnp.argsort(owners, stable=True)
    sorted_owners = owners[ordering]
    offsets = jnp.searchsorted(sorted_owners, jnp.arange(devices_all, dtype=jnp.int32), side="left")
    within = jnp.arange(marker_count, dtype=jnp.int32) - offsets[sorted_owners]
    places = (
        jnp.zeros((marker_count,), jnp.int32).at[ordering].set(sorted_owners * capacity + within)
    )
    described = three_factors(marker_coords)
    lead = described.shape[0]
    payload = jnp.concatenate([described, marker_force], axis=0)
    width_all = payload.shape[0]
    outgoing = jnp.zeros((width_all, slot_total), jnp.float32).at[:, places].set(payload)
    slot_ids = jnp.zeros((1, slot_total), jnp.int32).at[:, places].set(marker_element[None])
    got_floats, got_slots = (
        lax.all_to_all(
            outgoing.reshape(width_all, devices_all, capacity),
            ("gx", "gy"),
            split_axis=1,
            concat_axis=1,
            tiled=True,
        ),
        lax.all_to_all(
            slot_ids.reshape(1, devices_all, capacity),
            ("gx", "gy"),
            split_axis=1,
            concat_axis=1,
            tiled=True,
        ),
    )
    got_floats = got_floats.reshape(width_all, slot_total)
    element_ids = got_slots.reshape(slot_total)
    factors = got_floats[:lead]
    pushes = got_floats[lead:]
    block_len = math.gcd(slot_total, 512)
    block_count = slot_total // block_len
    factor_blocks = factors.reshape(3 * POINTS, block_count, block_len).transpose(1, 0, 2)
    element_blocks = element_ids.reshape(block_count, block_len)
    push_blocks = pushes.reshape(3, block_count, block_len).transpose(1, 0, 2)

    def sample(inputs):
        block_factors, block_elements = inputs
        weights = weight_table(block_factors)
        selector = selector_of(block_elements, elem_count)
        gathered = jnp.einsum("be,ken->kbn", selector, velocity, precision=lax.Precision.HIGHEST)
        return jnp.sum(gathered * weights[None], axis=-1)

    sampled = lax.map(sample, (factor_blocks, element_blocks))
    returning = sampled.transpose(1, 0, 2).reshape(3, slot_total)
    arrived = exchange_in_pieces(returning.reshape(3, devices_all, capacity), ("gx", "gy"), 2, 1, 1)

    def deposit(running, inputs):
        block_factors, block_elements, block_pushes = inputs
        weights = weight_table(block_factors)
        selector = selector_of(block_elements, elem_count)
        loads = block_pushes[:, :, None] * weights[None]
        added = jnp.einsum("be,kbn->ken", selector, loads, precision=lax.Precision.HIGHEST)
        return (running + added, None)

    node_forces, unused = lax.scan(
        deposit, jnp.zeros_like(velocity), (factor_blocks, element_blocks, push_blocks)
    )
    moved = jnp.take(arrived.reshape(3, slot_total), places, axis=1).reshape(positions.shape)
    return (positions + time_step * moved, node_forces)


def solution(mesh):
    return jax.shard_map(
        local,
        mesh=mesh,
        in_specs=(
            P(None, ("gx", "gy"), None),
            P(None, ("gx", "gy"), None),
            P(("gx", "gy"), None),
            P(("gx", "gy"), None),
            P(("gx", "gy"), None),
            P(("gx", "gy")),
            P(None, ("gx", "gy")),
        ),
        out_specs=(P(None, ("gx", "gy"), None), P(None, ("gx", "gy"), None)),
        check_vma=False,
    )
```

profile of v0, /device:TPU:1, one launch (start us, length us, event | category | flops | bytes accessed | tf_op | source)
XLA Modules:
  0.0 600.3 jit_solution(15195428008855210819)
XLA Ops:
  5.7 7.5 %sort.17 = (s32[8192]{0:T(1024)}, s32[8192]{0:T(1024)S(1)}) sort(s32[8192]{0:T(1024)} %bitcast.101, s32[8192]{0:T(1024)S(1)} %iota.23), dimensions={0}, to_apply=%region_0.1 | sort | flops 106496 | bytes 131072 | tf_op jit(solution)/shard_map/jit(argsort)/sort | solution.py:132
  13.3 45.5 %gather_fusion.1 = s32[8192]{0:T(1024)S(1)} fusion(s32[8192]{0:T(1024)S(1)} %bitcast.102, s32[8192]{0:T(1024)S(1)} %get-tuple-element.270), kind=kCustom, calls=%fused_computation.1 | custom fusion | bytes 98304 | tf_op jit(solution)/shard_map/gather | solution.py:133
  58.9 17.0 %while.46 = (s32[]{:T(128)}, u32[128]{0:T(128)S(1)}, u32[128]{0:T(128)S(1)}, s32[8192]{0:T(1024)S(1)}, s32[]{:T(128)}, /*index=5*/s32[]{:T(128)}, s32[]{}) while((s32[]{:T(128)}, u32[128]{0:T(128)S(1)}, u32[128]{0:T(128)S(1)}, s32[8192]{0:T(1024)S(1)}, s32[]{:T(128)}, /*index=5*/s32[]{:T(128)}, s32[]{}) %tuple.116), condition=%wide.region_2.3_spmd.clone, body=%wide.region_1.2_spmd.clone.sunk | while | flops 2692 | bytes 10340 | solution.py:134
  76.0 48.9 %gather_fusion.2 = s32[8192]{0:T(1024)S(1)} fusion(s32[128]{0:T(128)S(1)} %convert_element_type.17, s32[8192]{0:T(1024)S(1)} %broadcast_clamp_fusion.1), kind=kCustom, calls=%fused_computation.2 | custom fusion | bytes 98304 | tf_op jit(solution)/shard_map/gather | solution.py:135
  124.9 30.5 %scatter_custom_fusion = s32[8192]{0:T(1024)S(1)} fusion(s32[8192]{0:T(1024)S(1)} %get-tuple-element.271, s32[8192]{0:T(1024)S(1)} %subtract_add_fusion, s32[]{:T(128)} %constant.80.clone.1), kind=kCustom, calls=%fused_computation.253 | custom fusion | bytes 32772 | tf_op jit(solution)/shard_map/scatter | solution.py:137
  156.0 30.7 %scatter_custom_fusion.1 = s32[12288]{0:T(1024)S(1)} fusion(s32[8192]{0:T(1024)S(1)} %get-tuple-element.269, s32[8192]{0:T(1024)} %param.18, s32[]{:T(128)} %constant.80.clone.1), kind=kCustom, calls=%fused_computation.224 | custom fusion | bytes 49664 | tf_op jit(solution)/shard_map/scatter | solution.py:144
  187.3 9.3 %all-to-all-start = ((s32[1,128,96]{2,0,1:T(1,128)}), s32[1,128,96]{2,0,1:T(1,128)S(1)}, u32[]{:S(2)}, u32[]{:S(2)}) async-start(s32[1,128,96]{2,0,1:T(1,128)} %bitcast.14), calls=%async_computation | async-start | bytes 131072 | tf_op jit(solution)/shard_map/all_to_all | solution.py:153
  269.6 5.1 divide_multiply_fusion
  274.7 5.1 divide_multiply_fusion.6
  279.7 5.1 divide_multiply_fusion.12
  284.8 5.0 divide_multiply_fusion.18
  289.8 5.1 divide_multiply_fusion.24
  294.9 5.0 divide_multiply_fusion.30
  299.9 5.0 divide_multiply_fusion.36
  305.0 5.0 divide_multiply_fusion.42
  312.1 2.8 copy.72
  314.9 23.9 %scatter_custom_fusion.2 = f32[27,12288]{0,1:T(8,128)} fusion(s32[8192]{0:T(1024)S(1)} %get-tuple-element.269, f32[8192,27]{1,0:T(8,128)} %copy.72, f32[]{:T(128)} %constant.88.clone.1), kind=kCustom, calls=%fused_computation.42 | custom fusion | bytes 1327616 | tf_op jit(solution)/shard_map/scatter | solution.py:143
  338.8 5.9 copy.73
  344.7 10.2 %all-to-all-start.1 = ((f32[27,128,96]{2,0,1:T(8,128)}), f32[27,128,96]{2,0,1:T(8,128)}, u32[]{:S(2)}, u32[]{:S(2)}) async-start(f32[27,128,96]{2,0,1:T(8,128)} %copy.73), calls=%async_computation.1 | async-start | bytes 4194304 | tf_op jit(solution)/shard_map/all_to_all | solution.py:146
  356.8 28.3 %all-to-all-done.1 = f32[27,128,96]{2,0,1:T(8,128)} async-done(((f32[27,128,96]{2,0,1:T(8,128)}), f32[27,128,96]{2,0,1:T(8,128)}, u32[]{:S(2)}, u32[]{:S(2)}) %all-to-all-start.1) | async-done | bytes 1327136 | tf_op jit(solution)/shard_map/all_to_all | solution.py:146
  389.0 3.0 copy.76
  392.0 64.9 %while.45 = (s32[]{:T(128)}, f32[24,3,512]{2,1,0:T(4,128)S(1)}, s32[24,512]{1,0:T(8,128)S(1)}, f32[3,256,512]{1,2,0:T(8,128)S(1)}, f32[24,24,512]{2,1,0:T(8,128)}, /*index=5*/s32[]{:T(128)}, s32[]{:T(128)}, s32[]{}, s32[]{}) while((s32[]{:T(128)}, f32[24,3,512]{2,1,0:T(4,128)S(1)}, s32[24,512]{1,0:T(8,128)S(1)}, f32[3,256,512]{1,2,0:T(8,128)S(1)}, ...), condition=%wide.region_8.9_spmd, body=%wide.region_6.8_spmd.sunk | while | flops 2417916416 | bytes 4108425 | solution.py:178
  457.8 3.8 all-to-all-start.2
  463.7 7.5 %all-to-all-done.2 = f32[128,1,1,96]{3,1,2,0:T(1,128)S(1)} async-done(((f32[128,1,1,96]{3,1,2,0:T(1,128)}), f32[128,1,1,96]{3,1,2,0:T(1,128)S(1)}, u32[]{:S(2)}, u32[]{:S(2)}) %all-to-all-start.2) | async-done | bytes 49184 | tf_op jit(solution)/shard_map/all_to_all | solution.py:60
  471.2 4.2 all-to-all-start.3
  475.4 84.9 %while.47 = (s32[]{:T(128)}, f32[3,256,512]{1,2,0:T(8,128)S(1)}, f32[24,3,512]{2,0,1:T(8,128)S(1)}, f32[24,24,512]{2,1,0:T(8,128)}, s32[24,512]{1,0:T(8,128)S(1)}, /*index=5*/s32[]{:T(128)}, s32[]{:T(128)}, s32[]{}, s32[]{}) while((s32[]{:T(128)}, f32[3,256,512]{1,2,0:T(8,128)S(1)}, f32[24,3,512]{2,0,1:T(8,128)S(1)}, ...), condition=%wide.region_10.11_spmd.clone, body=%wide.region_9.10_spmd.clone.sunk | while | flops 2417917952 | bytes 5689491 | solution.py:190
  476.4 2.5 bitcast_add_fusion.2
  483.5 2.5 bitcast_add_fusion.2
  487.0 2.5 bitcast_add_fusion.2
  562.1 4.1 copy.80
  566.1 30.7 %gather_fusion.3 = f32[8192,3]{1,0:T(8,128)} fusion(f32[3,12288]{0,1:T(8,128)} %bitcast.107, s32[8192]{0:T(1024)S(1)} %copy-done.6), kind=kCustom, calls=%fused_computation.3 | custom fusion | bytes 229376 | tf_op jit(solution)/shard_map/jit(_take)/gather | solution.py:193
  596.8 2.8 copy.81
  (435 shorter events, 176.8 us)
Async XLA Ops:
  0.6 12.6 %copy-start = (s32[8192,1]{0,1:T(1,128)S(1)}, s32[8192,1]{0,1:T(1,128)}, u32[]{:S(2)}) copy-start(s32[8192,1]{0,1:T(1,128)} %param.17) | copy-start | bytes 98308
  1.4 308.6 %collective-permute-start.1 = (f32[4,2,256]{2,1,0:T(2,128)S(1)}, f32[4,2,256]{2,1,0:T(2,128)S(1)}, u32[]{:S(2)}, u32[]{:S(2)}) collective-permute-start(f32[4,2,256]{2,1,0:T(2,128)S(1)} %get-tuple-element.234), channel_id=1, source_target_pairs={{0,1},{1,2},{2,3},{3,4},{4,5},{5,6},{6,7},{7,8},{8,9},{9,10},{10,1... | collective-permute-start | bytes 24584 | tf_op jit(solution)/shard_map/ppermute | solution.py:23
  3.6 306.4 %collective-permute-start = (f32[4,2,256]{2,1,0:T(2,128)S(1)}, f32[4,2,256]{2,1,0:T(2,128)S(1)}, u32[]{:S(2)}, u32[]{:S(2)}) collective-permute-start(f32[4,2,256]{2,1,0:T(2,128)S(1)} %get-tuple-element.235), channel_id=1, source_target_pairs={{1,0},{2,1},{3,2},{4,3},{5,4},{6,5},{7,6},{8,7},{9,8},{10,9},{11,1... | collective-permute-start | bytes 24584 | tf_op jit(solution)/shard_map/ppermute | solution.py:24
  75.9 120.8 %copy-start.1 = (f32[3,32,256]{2,1,0:T(8,128)S(1)}, f32[3,32,256]{2,1,0:T(8,128)}, u32[]{:S(2)}) copy-start(f32[3,32,256]{2,1,0:T(8,128)} %param.14) | copy-start | bytes 294916
  75.9 193.6 %copy-start.5 = (f32[32,256]{1,0:T(8,128)S(1)}, f32[32,256]{1,0:T(8,128)}, u32[]{:S(2)}) copy-start(f32[32,256]{1,0:T(8,128)} %param.15) | copy-start | bytes 98308
  75.9 193.7 %copy-start.2 = (f32[3,8192]{1,0:T(4,128)S(1)}, f32[3,8192]{1,0:T(4,128)}, u32[]{:S(2)}) copy-start(f32[3,8192]{1,0:T(4,128)} %param.19) | copy-start | bytes 294916
  124.8 185.2 %copy-start.4 = (f32[32,256]{1,0:T(8,128)S(1)}, f32[32,256]{1,0:T(8,128)}, u32[]{:S(2)}) copy-start(f32[32,256]{1,0:T(8,128)} %param.16) | copy-start | bytes 98308
  187.3 157.3 %all-to-all-start = ((s32[1,128,96]{2,0,1:T(1,128)}), s32[1,128,96]{2,0,1:T(1,128)S(1)}, u32[]{:S(2)}, u32[]{:S(2)}) async-start(s32[1,128,96]{2,0,1:T(1,128)} %bitcast.14), calls=%async_computation | async-start | bytes 131072 | tf_op jit(solution)/shard_map/all_to_all | solution.py:153
  344.7 10.3 %copy-start.3 = (f32[3,256,512]{2,1,0:T(8,128)S(1)}, f32[3,256,512]{2,1,0:T(8,128)}, u32[]{:S(2)}) copy-start(f32[3,256,512]{2,1,0:T(8,128)} %param.13) | copy-start | bytes 4718596
  344.7 40.4 %all-to-all-start.1 = ((f32[27,128,96]{2,0,1:T(8,128)}), f32[27,128,96]{2,0,1:T(8,128)}, u32[]{:S(2)}, u32[]{:S(2)}) async-start(f32[27,128,96]{2,0,1:T(8,128)} %copy.73), calls=%async_computation.1 | async-start | bytes 4194304 | tf_op jit(solution)/shard_map/all_to_all | solution.py:146
  457.8 13.4 %all-to-all-start.2 = ((f32[128,1,1,96]{3,1,2,0:T(1,128)}), f32[128,1,1,96]{3,1,2,0:T(1,128)S(1)}, u32[]{:S(2)}, u32[]{:S(2)}) async-start(f32[128,1,1,96]{3,1,2,0:T(1,128)} %bitcast.30), calls=%async_computation.2 | async-start | bytes 131072 | tf_op jit(solution)/shard_map/all_to_all | solution.py:60
  471.2 90.7 %all-to-all-start.3 = ((f32[128,2,1,96]{3,1,2,0:T(2,128)}), f32[128,2,1,96]{3,1,2,0:T(2,128)S(1)}, u32[]{:S(2)}, u32[]{:S(2)}) async-start(f32[128,2,1,96]{3,1,2,0:T(2,128)} %copy.79), calls=%async_computation.3 | async-start | bytes 262144 | tf_op jit(solution)/shard_map/all_to_all | solution.py:60
  562.1 4.1 copy-start.6
where the time goes:
time: 610 us; the launch traced here: 600 us
  local copies, waits for them, and re-layouts  296 us (49%)
  matrix products  103 us (17%)
  between operations  73 us (12%)
  other arithmetic  58.4 us (10%)
  waiting for transfers between devices  35.8 us (6%)
  starting transfers between devices  31.8 us (5%)
    dot_general x24, matrix products, deposit(): jnp.einsum('be,kbn->ken', selector, loads, precision=lax.Precision.HIGHEST)  60.9 us
    gather x1, local copies, waits for them, and re-layouts, local(): within = jnp.arange(marker_count, dtype=jnp.int32) - offsets[sorted_owners]  48.9 us
    gather x1, local copies, waits for them, and re-layouts, local(): sorted_owners = owners[ordering]  45.5 us
    dot_general x24, matrix products, sample(): jnp.einsum('be,ken->kbn', selector, velocity, precision=lax.Precision.HIG...  41.8 us
    mul x8, other arithmetic, basis(): product = product * ((values - abscissa[j]) / (abscissa[i] - abscissa[j]))  40.3 us
    transpose x48, local copies, waits for them, and re-layouts, weight_table(): along_r = factors[0:POINTS].T  36.7 us
    gather x2, local copies, waits for them, and re-layouts, local(): jnp.take(arrived.reshape(3, slot_total), places, axis=1)  33.5 us
    scatter x1, local copies, waits for them, and re-layouts, local(): jnp.zeros((1, slot_total), jnp.int32).at[:, places]  30.7 us
  transfers between devices with their start and end apart: 6, of which 2 were waited for; matrix products, arithmetic and copies ran while one was open for 58% of the time, Pallas kernels for 0%

commit v1 on v0

v1 whole, which is shorter than its diff:
```python
import math

import jax
import jax.numpy as jnp
import numpy as np
from jax import lax
from jax.experimental import pallas as pl
from jax.experimental.pallas import tpu as pltpu
from jax.sharding import PartitionSpec as P

POINTS = 8
NODES = 512
ELEMS = 256
ROWS = 32
COLS = 256
DEVICES = 128
LANES = 128
HALF = 64
TILES = 96
CHUNK = 512
CHUNK_TILES = CHUNK // LANES
COMP_TILES = 100

bend_modulus = 0.05
time_step = 0.5

BF = jnp.bfloat16
F32 = jnp.float32
I32 = jnp.int32
NN = (((1,), (0,)), ((), ()))
NT = (((1,), (1,)), ((), ()))


def dot(a, b, dims=NN):
    return lax.dot_general(a, b, dims, preferred_element_type=F32)


def iota(shape, dim):
    return lax.broadcasted_iota(I32, shape, dim)


def one_hot(row, count):
    hit = jnp.broadcast_to(row, (count, row.shape[1])) == iota((count, row.shape[1]), 0)
    return jnp.where(hit, 1.0, 0.0).astype(BF)


def split(x):
    high = x.astype(BF)
    return high, (x - high.astype(F32)).astype(BF)


def basis_tables():
    nodes = -np.cos(np.pi * np.arange(POINTS, dtype=np.float64) / (POINTS - 1))
    nodes = nodes.astype(np.float32).astype(np.float64)
    scale = np.zeros((POINTS, POINTS))
    for j in range(POINTS):
        for i in range(POINTS):
            if i != j:
                scale[j, i] = 1.0 / (nodes[i] - nodes[j])
    scale = np.broadcast_to(scale[:, :, None], (POINTS, POINTS, LANES))
    return nodes, np.ascontiguousarray(scale, np.float32)


NODE_AT, SCALE_OF = basis_tables()


def basis(row, scale):
    n = row.shape[1]
    x = jnp.broadcast_to(row, (POINTS, n))
    which = iota((POINTS, n), 0)
    product = None
    for j in range(POINTS):
        s = jnp.concatenate([scale[j]] * (n // LANES), axis=1)
        factor = jnp.where(which == j, 1.0, (x - float(NODE_AT[j])) * s)
        product = factor if product is None else product * factor
    return product


def dispatch(below, above, positions, stiff_h, stiff_v, owner, element, coords,
             send, slot, ext, vals, pre, cnt, acc):
    ext[:, 8:8 + ROWS] = jnp.concatenate([positions[...], stiff_v[...][None]], axis=0)
    ext[:, 6:8] = below[...]
    ext[:, 8 + ROWS:10 + ROWS] = above[...]

    def rows(k, first, count):
        return ext[k, first + 8:first + 8 + count]

    sh = stiff_h[...]
    sh_left = pltpu.roll(sh, 1, 1)
    sv = rows(3, 0, ROWS)
    sv_below = rows(3, -1, ROWS)
    for k in range(3):
        mid = rows(k, 0, ROWS)
        pull = (
            sh * (pltpu.roll(mid, COLS - 1, 1) - mid)
            + sh_left * (pltpu.roll(mid, 1, 1) - mid)
            + sv * (rows(k, 1, ROWS) - mid)
            + sv_below * (rows(k, -1, ROWS) - mid)
        )

        def lap_at(first):
            m = rows(k, first, ROWS)
            return (
                rows(k, first + 1, ROWS)
                + rows(k, first - 1, ROWS)
                + pltpu.roll(m, 1, 1)
                + pltpu.roll(m, COLS - 1, 1)
                - 4.0 * m
            )

        lap = lap_at(0)
        bend = (
            lap_at(1)
            + lap_at(-1)
            + pltpu.roll(lap, 1, 1)
            + pltpu.roll(lap, COLS - 1, 1)
            - 4.0 * lap
        )
        force = pull - bend_modulus * bend
        c = coords[k]
        for i, v in ((k, c), (3 + k, force)):
            high = v.astype(BF).astype(F32)
            vals[2 * i] = high
            vals[2 * i + 1] = v - high
    vals[12] = element[...].astype(F32)

    before = jnp.where(iota((COLS, COLS), 0) < iota((COLS, COLS), 1), 1.0, 0.0).astype(BF)
    table = jnp.concatenate([before, jnp.ones((COLS, LANES), BF)], axis=1)

    @pl.loop(0, ROWS, unroll=4)
    def _(r):
        hot = one_hot(owner[pl.ds(r, 1), :], DEVICES)
        p = dot(hot, table)
        pre[r] = p[:, :COLS]
        cnt[r] = p[:, COLS:]

    def rank_rows(r, base):
        own = owner[pl.ds(r, 1), :]
        hit = jnp.broadcast_to(own, (DEVICES, COLS)) == iota((DEVICES, COLS), 0)
        both = jnp.concatenate([base, base], axis=1)
        rank = jnp.sum(jnp.where(hit, pre[r] + both, 0.0), axis=0, keepdims=True)
        slot[pl.ds(r, 1), :] = own * LANES + rank.astype(I32)
        return base + cnt[r]

    total = lax.fori_loop(0, ROWS, rank_rows, jnp.zeros((DEVICES, LANES), F32), unroll=4)

    acc[...] = jnp.zeros_like(acc)

    @pl.loop(0, ROWS, unroll=2)
    def _(r):
        p = slot[pl.ds(r, 1), :]
        low = one_hot(jnp.bitwise_and(p, 255), 256)
        hit = jnp.broadcast_to(lax.shift_right_logical(p, 8), (HALF, COLS)) == iota((HALF, COLS), 0)

        def picked(i):
            row = jnp.broadcast_to(vals[i, pl.ds(r, 1), :], (HALF, COLS))
            return jnp.where(hit, row, 0.0).astype(BF)

        highs = jnp.concatenate([picked(2 * i) for i in range(7)], axis=0)
        lows = jnp.concatenate([picked(2 * i + 1) for i in range(6)], axis=0)
        acc[:6 * HALF] += dot(highs[:6 * HALF], low, NT) + dot(lows, low, NT)
        acc[6 * HALF:] += dot(highs[6 * HALF:], low, NT)

    for i in range(7):
        v = acc[i * HALF:(i + 1) * HALF]
        send[:, i, :] = v[:, :LANES]
        send[:, 8 + i, :] = v[:, LANES:]
    cnt[0] = total
    send[:, 7, :] = cnt[0, pl.ds(0, HALF, stride=2), :]
    send[:, 15, :] = cnt[0, pl.ds(1, HALF, stride=2), :]


def run_dispatch(below, above, positions, stiff_h, stiff_v, owner, element, coords):
    return pl.pallas_call(
        dispatch,
        out_shape=(
            jax.ShapeDtypeStruct((HALF, 16, LANES), F32),
            jax.ShapeDtypeStruct((ROWS, COLS), I32),
        ),
        in_specs=[pl.BlockSpec(memory_space=pltpu.VMEM)] * 8,
        out_specs=(pl.BlockSpec(memory_space=pltpu.VMEM),) * 2,
        scratch_shapes=[
            pltpu.VMEM((4, ROWS + 16, COLS), F32),
            pltpu.VMEM((13, ROWS, COLS), F32),
            pltpu.VMEM((ROWS, DEVICES, COLS), F32),
            pltpu.VMEM((ROWS, DEVICES, LANES), F32),
            pltpu.VMEM((7 * HALF, COLS), F32),
        ],
        name="dispatch",
    )(below, above, positions, stiff_h, stiff_v, owner, element, coords)


def tile_rows(comp, first, value):
    return jnp.concatenate([comp[first + t, value:value + 1, :] for t in range(CHUNK_TILES)], axis=1)


def sample(recv, velocity, scale, back, comp, total, vt, sampled, offs_v, offs, sem):
    counts = recv[:, 7, :]
    by_lane = jnp.transpose(counts)[:8].astype(BF)
    upto = jnp.where(iota((LANES, LANES), 0) < iota((LANES, LANES), 1), 1.0, 0.0).astype(BF)
    whole = jnp.ones((LANES, LANES), BF)
    offs_v[...] = jnp.concatenate([dot(by_lane, upto), dot(by_lane, whole)], axis=0).astype(I32)
    copy = pltpu.make_async_copy(offs_v, offs, sem)
    copy.start()
    for k in range(3):
        high, low = split(jnp.transpose(velocity[k]))
        vt[k * NODES:(k + 1) * NODES, :ELEMS] = high
        vt[k * NODES:(k + 1) * NODES, ELEMS:] = low
    copy.wait()
    comp[0] = jnp.zeros((8, LANES), F32)
    lane = iota((8, LANES), 1)

    @pl.loop(0, DEVICES, unroll=8)
    def _(s):
        off = offs[0, s]
        turn = jnp.bitwise_and(off, LANES - 1)
        first = lax.shift_right_logical(off, 7)
        turned = pltpu.roll(recv[s], turn, 1)
        comp[first] = comp[first] + jnp.where(lane >= turn, turned, 0.0)
        comp[first + 1] = jnp.where(lane < turn, turned, 0.0)

    count = offs[8, 0]
    total[0] = count
    used = lax.shift_right_logical(count + (LANES - 1), 7)
    for t in range(CHUNK_TILES):
        comp[used + t] = jnp.zeros((8, LANES), F32)
    steps = lax.shift_right_logical(count + (CHUNK - 1), int(math.log2(CHUNK)))
    table = scale[...]

    @pl.loop(0, steps)
    def _(j):
        first = j * CHUNK_TILES
        hot = one_hot(tile_rows(comp, first, 6).astype(I32), ELEMS)
        hot2 = jnp.concatenate([hot, hot], axis=0)
        along_r = basis(tile_rows(comp, first, 0), table)
        along_s = basis(tile_rows(comp, first, 1), table)
        along_t = basis(tile_rows(comp, first, 2), table)
        out = []
        for k in range(3):
            gk = dot(vt[k * NODES:(k + 1) * NODES, :], hot2)
            over_r = None
            for a in range(POINTS):
                term = gk[a * 64:(a + 1) * 64] * along_r[a:a + 1]
                over_r = term if over_r is None else over_r + term
            over_s = None
            for b in range(POINTS):
                term = over_r[b * 8:(b + 1) * 8] * along_s[b:b + 1]
                over_s = term if over_s is None else over_s + term
            out.append(jnp.sum(over_s * along_t, axis=0, keepdims=True))
        for t in range(CHUNK_TILES):
            for k in range(3):
                sampled[first + t, k:k + 1, :] = out[k][:, t * LANES:(t + 1) * LANES]

    sampled[used] = jnp.zeros((4, LANES), F32)
    sampled[used + 1] = jnp.zeros((4, LANES), F32)
    lane4 = iota((4, LANES), 1)

    @pl.loop(0, DEVICES, unroll=8)
    def _(s):
        off = offs[0, s]
        turn = jnp.bitwise_and(off, LANES - 1)
        first = lax.shift_right_logical(off, 7)
        both = jnp.where(lane4 >= turn, sampled[first], sampled[first + 1])
        back[s] = pltpu.roll(both, jnp.bitwise_and(LANES - turn, LANES - 1), 1)


def run_sample(recv, velocity):
    return pl.pallas_call(
        sample,
        out_shape=(
            jax.ShapeDtypeStruct((DEVICES, 4, LANES), F32),
            jax.ShapeDtypeStruct((COMP_TILES, 8, LANES), F32),
            jax.ShapeDtypeStruct((1,), I32),
        ),
        in_specs=[pl.BlockSpec(memory_space=pltpu.VMEM)] * 3,
        out_specs=(
            pl.BlockSpec(memory_space=pltpu.VMEM),
            pl.BlockSpec(memory_space=pltpu.VMEM),
            pl.BlockSpec(memory_space=pltpu.SMEM),
        ),
        scratch_shapes=[
            pltpu.VMEM((3 * NODES, 2 * ELEMS), BF),
            pltpu.VMEM((COMP_TILES, 4, LANES), F32),
            pltpu.VMEM((16, LANES), I32),
            pltpu.SMEM((16, LANES), I32),
            pltpu.SemaphoreType.DMA,
        ],
        name="sample",
    )(recv, velocity, jnp.asarray(SCALE_OF))


def deposit(total, comp, scale, out, acc, loads):
    acc[...] = jnp.zeros_like(acc)
    steps = lax.shift_right_logical(total[0] + (CHUNK - 1), int(math.log2(CHUNK)))
    table = scale[...]

    @pl.loop(0, steps)
    def _(j):
        first = j * CHUNK_TILES
        hot = one_hot(tile_rows(comp, first, 6).astype(I32), ELEMS)
        hot2 = jnp.concatenate([hot, hot], axis=1)
        along_r = basis(tile_rows(comp, first, 0), table)
        along_s = basis(tile_rows(comp, first, 1), table)
        along_t = basis(tile_rows(comp, first, 2), table)
        plane = jnp.concatenate([along_s[b:b + 1] * along_t for b in range(POINTS)], axis=0)
        for k in range(3):
            push = along_r * tile_rows(comp, first, 3 + k)
            for a in range(POINTS):
                high, low = split(plane * push[a:a + 1])
                at = k * NODES + a * 64
                loads[at:at + 64, :CHUNK] = high
                loads[at:at + 64, CHUNK:] = low
            at = k * NODES
            acc[at:at + NODES] += dot(loads[at:at + NODES], hot2, NT)

    for k in range(3):
        out[k] = jnp.transpose(acc[k * NODES:(k + 1) * NODES])


def run_deposit(total, comp):
    return pl.pallas_call(
        deposit,
        out_shape=jax.ShapeDtypeStruct((3, ELEMS, NODES), F32),
        in_specs=[
            pl.BlockSpec(memory_space=pltpu.SMEM),
            pl.BlockSpec(memory_space=pltpu.VMEM),
            pl.BlockSpec(memory_space=pltpu.VMEM),
        ],
        out_specs=pl.BlockSpec(memory_space=pltpu.VMEM),
        scratch_shapes=[pltpu.VMEM((3 * NODES, ELEMS), F32), pltpu.VMEM((3 * NODES, 2 * CHUNK), BF)],
        name="deposit",
    )(total, comp, jnp.asarray(SCALE_OF))


def collect(got, slot, positions, out, table):
    for k in range(3):
        both = jnp.concatenate([got[:, k, :], got[:, 4 + k, :]], axis=1)
        high, low = split(both)
        table[k * HALF:(k + 1) * HALF, :COLS] = high
        table[k * HALF:(k + 1) * HALF, COLS:] = low

    @pl.loop(0, ROWS, unroll=4)
    def _(r):
        p = slot[pl.ds(r, 1), :]
        low = one_hot(jnp.bitwise_and(p, 255), 256)
        hit = jnp.broadcast_to(lax.shift_right_logical(p, 8), (HALF, COLS)) == iota((HALF, COLS), 0)
        g = dot(table[...], jnp.concatenate([low, low], axis=0))
        for k in range(3):
            mine = jnp.sum(jnp.where(hit, g[k * HALF:(k + 1) * HALF], 0.0), axis=0, keepdims=True)
            out[k, pl.ds(r, 1), :] = positions[k, pl.ds(r, 1), :] + time_step * mine


def run_collect(got, slot, positions):
    return pl.pallas_call(
        collect,
        out_shape=jax.ShapeDtypeStruct((3, ROWS, COLS), F32),
        in_specs=[pl.BlockSpec(memory_space=pltpu.VMEM)] * 3,
        out_specs=pl.BlockSpec(memory_space=pltpu.VMEM),
        scratch_shapes=[pltpu.VMEM((3 * HALF, 2 * COLS), BF)],
        name="collect",
    )(got, slot, positions)


def edges(positions, stiff_v):
    stacked = jnp.concatenate([positions, stiff_v[None]], axis=0)
    axes = ("gx", "gy")
    peers = lax.axis_size("gx") * lax.axis_size("gy")
    up = [(i, (i + 1) % peers) for i in range(peers)]
    below = lax.ppermute(stacked[:, ROWS - 2:], axes, up)
    above = lax.ppermute(stacked[:, :2], axes, [(b, a) for a, b in up])
    return below, above


def local(velocity, positions, stiff_h, stiff_v, marker_owner, marker_element, marker_coords):
    owner = marker_owner.reshape(ROWS, COLS)
    element = marker_element.reshape(ROWS, COLS)
    coords = marker_coords.reshape(3, ROWS, COLS)
    below, above = edges(positions, stiff_v)
    send, slot = run_dispatch(below, above, positions, stiff_h, stiff_v, owner, element, coords)
    recv = lax.all_to_all(
        send.reshape(DEVICES, 8, LANES), ("gx", "gy"), split_axis=0, concat_axis=0, tiled=True
    )
    back, comp, total = run_sample(recv, velocity)
    got = lax.all_to_all(back, ("gx", "gy"), split_axis=0, concat_axis=0, tiled=True)
    node_forces = run_deposit(total, comp)
    moved = run_collect(got.reshape(HALF, 8, LANES), slot, positions)
    return moved, node_forces


def solution(mesh):
    return jax.shard_map(
        local,
        mesh=mesh,
        in_specs=(
            P(None, ("gx", "gy"), None),
            P(None, ("gx", "gy"), None),
            P(("gx", "gy"), None),
            P(("gx", "gy"), None),
            P(("gx", "gy"), None),
            P(("gx", "gy")),
            P(None, ("gx", "gy")),
        ),
        out_specs=(P(None, ("gx", "gy"), None), P(None, ("gx", "gy"), None)),
        check_vma=False,
    )
```

time: 610 us -> 122 us (0.20)
  the two profiles are of different devices: /device:TPU:1 before, /device:TPU:34 now
where the time goes in v1:
time: 122 us; the launch traced here: 120 us
  Pallas kernels  78 us (64%)
  blocking collectives  26.1 us (21%)
  starting transfers between devices  8.06 us (7%)
  local copies, waits for them, and re-layouts  5.34 us (4%)
  other arithmetic  2.28 us (2%)
    pallas_call x1, Pallas kernels, run_sample(): pl.pallas_call(sample, out_shape=(jax.ShapeDtypeStruct((DEVICES, 4, LANES...  30.6 us
    pallas_call x1, Pallas kernels, run_deposit(): pl.pallas_call(deposit, out_shape=jax.ShapeDtypeStruct((3, ELEMS, NODES),...  28.2 us
    all_to_all x1, blocking collectives, local(): lax.all_to_all(send.reshape(DEVICES, 8, LANES), ('gx', 'gy'), split_axis=...  26.1 us
    pallas_call x1, Pallas kernels, run_dispatch(): pl.pallas_call(dispatch, out_shape=(jax.ShapeDtypeStruct((HALF, 16, LANES...  13.9 us
    all_to_all x1, starting transfers between devices, local(): lax.all_to_all(back, ('gx', 'gy'), split_axis=0, concat_axis=0, tiled=True)  5.57 us
    pallas_call x1, Pallas kernels, run_collect(): pl.pallas_call(collect, out_shape=jax.ShapeDtypeStruct((3, ROWS, COLS), F...  5.32 us
    unnamed x8, local copies, waits for them, and re-layouts  3.36 us
    ppermute x1, starting transfers between devices, edges(): above = lax.ppermute(stacked[:, :2], axes, [(b, a) for a, b in up])  2.49 us
  transfers between devices with their start and end apart: 3, of which 0 were waited for; matrix products, arithmetic and copies ran while one was open for 5% of the time, Pallas kernels for 23%

profile of v1, /device:TPU:34, one launch (start us, length us, event | category | flops | bytes accessed | tf_op | source)
XLA Modules:
  0.0 120.5 jit_solution(12736371120124376408)
XLA Ops:
  0.6 0.8 pad_maximum_fusion
  1.4 2.5 %collective-permute-start.1 = (f32[4,2,256]{2,1,0:T(2,128)S(1)}, f32[4,2,256]{2,1,0:T(2,128)S(1)}, u32[]{:S(2)}, u32[]{:S(2)}) collective-permute-start(f32[4,2,256]{2,1,0:T(2,128)S(1)} %get-tuple-element.12), channel_id=1, source_target_pairs={{1,0},{2,1},{3,2},{4,3},{5,4},{6,5},{7,6},{8,7},{9,8},{10,9},{11,1... | collective-permute-start | bytes 24584 | tf_op jit(solution)/shard_map/ppermute | solution.py:370
  3.9 0.0 collective-permute-start
  3.9 0.5 broadcast.3
  4.4 1.5 %reduce.3 = s32[8192]{0:T(1024)S(1)} reduce(s32[8192,1]{0,1:T(1,128)} %param.12, s32[]{:T(128)} %broadcast.3), dimensions={1}, to_apply=%param.12.reduce_sub_computation.3 | reduce | bytes 65540 | tf_op args[4]
  5.9 0.6 reshape.19.owner
  6.5 1.4 %reshape.20.element = s32[32,256]{1,0:T(8,128)} reshape(s32[8192]{0:T(1024)} %param.13) | data formatting | bytes 65536 | tf_op jit(solution)/shard_map/reshape | solution.py:376
  7.9 1.6 %copy.12 = f32[1,3,32,256]{3,2,1,0:T(8,128)} copy(f32[1,3,32,256]{3,1,2,0:T(4,128)} %bitcast.11) | data formatting | bytes 196608
  9.5 0.0 collective-permute-done.1.above
  9.5 0.0 copy-start.1
  9.5 0.0 collective-permute-done.below
  9.5 0.0 copy-start.2
  9.5 0.6 copy-done.1
  10.1 0.0 copy-done.2
  10.1 13.9 %dispatch.1 = (f32[64,16,128]{2,1,0:T(8,128)}, s32[32,256]{1,0:T(8,128)}) custom-call(f32[4,2,256]{2,1,0:T(2,128)} %copy-done.2, f32[4,2,256]{2,1,0:T(2,128)} %copy-done.1, f32[3,32,256]{2,1,0:T(8,128)} %positions.3, f32[32,256]{1,0:T(8,128)} %stiff_h.1, f32[32,256]{1,0:T(8,128)} %stiff_v.1, s32[32,256]{1,0:T(8,128)} %reshape.19.owner, ...), custom_call_target="tpu_custom_call" | custom-call | tf_op jit(solution)/shard_map/dispatch/pallas_call | solution.py:174
  24.0 26.1 %all_to_all.10.recv = f32[128,8,128]{2,1,0:T(8,128)} all-to-all(f32[128,8,128]{2,1,0:T(8,128)} %bitcast.9), channel_id=1, replica_groups=mesh['gx'=32,'gy'=4] {'gx','gy'}, dimensions={0} | all-to-all | bytes 1048576 | tf_op jit(solution)/shard_map/all_to_all | solution.py:380
  50.0 30.6 %sample.1 = (f32[128,4,128]{2,1,0:T(4,128)}, f32[100,8,128]{2,1,0:T(8,128)}, s32[1]{0:T(128)}) custom-call(f32[128,8,128]{2,1,0:T(8,128)} %all_to_all.10.recv, f32[3,256,512]{2,1,0:T(8,128)} %velocity.1, f32[8,8,128]{2,1,0:T(8,128)} %constant.2.clone.scale), custom_call_target="tpu_custom_call" | custom-call | tf_op jit(solution)/shard_map/sample/pallas_call | solution.py:268
  80.6 5.6 %all-to-all-start.1 = ((f32[128,4,128]{2,1,0:T(4,128)}), f32[128,4,128]{2,1,0:T(4,128)S(1)}, u32[]{:S(2)}, u32[]{:S(2)}) async-start(f32[128,4,128]{2,1,0:T(4,128)} %get-tuple-element.8), calls=%async_computation.1 | async-start | bytes 524288 | tf_op jit(solution)/shard_map/all_to_all | solution.py:384
  86.2 28.2 %deposit.1 = f32[3,256,512]{2,1,0:T(8,128)} custom-call(s32[1]{0:T(128)} %get-tuple-element.10.total, f32[100,8,128]{2,1,0:T(8,128)} %get-tuple-element.11.comp, f32[8,8,128]{2,1,0:T(8,128)} %constant.2.clone.scale), custom_call_target="tpu_custom_call" | custom-call | tf_op jit(solution)/shard_map/deposit/pallas_call | solution.py:321
  114.4 0.0 all-to-all-done.1
  114.4 0.0 copy-start
  114.4 0.7 copy-done
  115.1 5.3 %collect.1 = f32[3,32,256]{2,1,0:T(8,128)} custom-call(f32[64,8,128]{2,1,0:T(8,128)} %bitcast.8, s32[32,256]{1,0:T(8,128)} %get-tuple-element.9.slot, f32[3,32,256]{2,1,0:T(8,128)} %positions.3), custom_call_target="tpu_custom_call" | custom-call | tf_op jit(solution)/shard_map/collect/pallas_call | solution.py:354
Async XLA Ops:
  1.4 8.0 %collective-permute-start.1 = (f32[4,2,256]{2,1,0:T(2,128)S(1)}, f32[4,2,256]{2,1,0:T(2,128)S(1)}, u32[]{:S(2)}, u32[]{:S(2)}) collective-permute-start(f32[4,2,256]{2,1,0:T(2,128)S(1)} %get-tuple-element.12), channel_id=1, source_target_pairs={{1,0},{2,1},{3,2},{4,3},{5,4},{6,5},{7,6},{8,7},{9,8},{10,9},{11,1... | collective-permute-start | bytes 24584 | tf_op jit(solution)/shard_map/ppermute | solution.py:370
  3.9 5.6 %collective-permute-start = (f32[4,2,256]{2,1,0:T(2,128)S(1)}, f32[4,2,256]{2,1,0:T(2,128)S(1)}, u32[]{:S(2)}, u32[]{:S(2)}) collective-permute-start(f32[4,2,256]{2,1,0:T(2,128)S(1)} %get-tuple-element.13), channel_id=1, source_target_pairs={{0,1},{1,2},{2,3},{3,4},{4,5},{5,6},{6,7},{7,8},{8,9},{9,10},{10,1... | collective-permute-start | bytes 24584 | tf_op jit(solution)/shard_map/ppermute | solution.py:369
  9.5 0.6 copy-start.1
  9.5 0.6 copy-start.2
  80.6 33.8 %all-to-all-start.1 = ((f32[128,4,128]{2,1,0:T(4,128)}), f32[128,4,128]{2,1,0:T(4,128)S(1)}, u32[]{:S(2)}, u32[]{:S(2)}) async-start(f32[128,4,128]{2,1,0:T(4,128)} %get-tuple-element.8), calls=%async_computation.1 | async-start | bytes 524288 | tf_op jit(solution)/shard_map/all_to_all | solution.py:384
  114.4 0.7 copy-start

commit v2 on v1

v2 whole, which is shorter than its diff:
```python
import math

import jax
import jax.numpy as jnp
import numpy as np
from jax import lax
from jax.experimental import pallas as pl
from jax.experimental.pallas import tpu as pltpu
from jax.sharding import PartitionSpec as P

POINTS = 8
NODES = 512
ELEMS = 256
ROWS = 32
COLS = 256
DEVICES = 128
LANES = 128
HALF = 64
TILES = 96
CHUNK = 512
CHUNK_TILES = CHUNK // LANES
CAP = 96
GROUPS = 8
PER_GROUP = DEVICES // GROUPS

bend_modulus = 0.05
time_step = 0.5

BF = jnp.bfloat16
F32 = jnp.float32
I32 = jnp.int32
NN = (((1,), (0,)), ((), ()))
NT = (((1,), (1,)), ((), ()))


def dot(a, b, dims=NN):
    return lax.dot_general(a, b, dims, preferred_element_type=F32)


def iota(shape, dim):
    return lax.broadcasted_iota(I32, shape, dim)


def one_hot(row, count):
    hit = jnp.broadcast_to(row, (count, row.shape[1])) == iota((count, row.shape[1]), 0)
    return jnp.where(hit, 1.0, 0.0).astype(BF)


def split(x):
    high = x.astype(BF)
    return high, (x - high.astype(F32)).astype(BF)


def basis_tables():
    nodes = -np.cos(np.pi * np.arange(POINTS, dtype=np.float64) / (POINTS - 1))
    nodes = nodes.astype(np.float32).astype(np.float64)
    scale = np.zeros((POINTS, POINTS))
    for j in range(POINTS):
        for i in range(POINTS):
            if i != j:
                scale[j, i] = 1.0 / (nodes[i] - nodes[j])
    scale = np.broadcast_to(scale[:, :, None], (POINTS, POINTS, LANES))
    return nodes, np.ascontiguousarray(scale, np.float32)


NODE_AT, SCALE_OF = basis_tables()


def basis(row, scale):
    n = row.shape[1]
    x = jnp.broadcast_to(row, (POINTS, n))
    which = iota((POINTS, n), 0)
    product = None
    for j in range(POINTS):
        s = jnp.concatenate([scale[j]] * (n // LANES), axis=1)
        factor = jnp.where(which == j, 1.0, (x - float(NODE_AT[j])) * s)
        product = factor if product is None else product * factor
    return product

MESH = pl.DeviceIdType.MESH


def place(index):
    return (index // 4, index % 4)


def tile_rows(comp, first, value):
    return jnp.concatenate([comp[first + t, value:value + 1, :] for t in range(CHUNK_TILES)], axis=1)


def forces(ext, stiff_h, vals):
    def rows(k, first, count):
        return ext[k, first + 8:first + 8 + count]

    sh = stiff_h[...]
    sh_left = pltpu.roll(sh, 1, 1)
    sv = rows(3, 0, ROWS)
    sv_below = rows(3, -1, ROWS)
    for k in range(3):
        mid = rows(k, 0, ROWS)
        pull = (
            sh * (pltpu.roll(mid, COLS - 1, 1) - mid)
            + sh_left * (pltpu.roll(mid, 1, 1) - mid)
            + sv * (rows(k, 1, ROWS) - mid)
            + sv_below * (rows(k, -1, ROWS) - mid)
        )

        def lap_at(first):
            m = rows(k, first, ROWS)
            return (
                rows(k, first + 1, ROWS)
                + rows(k, first - 1, ROWS)
                + pltpu.roll(m, 1, 1)
                + pltpu.roll(m, COLS - 1, 1)
                - 4.0 * m
            )

        lap = lap_at(0)
        bend = (
            lap_at(1)
            + lap_at(-1)
            + pltpu.roll(lap, 1, 1)
            + pltpu.roll(lap, COLS - 1, 1)
            - 4.0 * lap
        )
        force = pull - bend_modulus * bend
        high = force.astype(BF).astype(F32)
        vals[2 * k] = high
        vals[2 * k + 1] = force - high


def step(positions, stiff_h, stiff_v, owner, element, coords, velocity, scale,
         moved, out,
         ext, halo, vals, slot, acc, send, recv, comp, sampled, back, got, table,
         vel, vt, force_acc, loads,
         vel_sem, halo_send, halo_recv, send_sem, recv_sem, back_send, back_recv):
    me = lax.axis_index("gx") * 4 + lax.axis_index("gy")
    up, down = lax.rem(me + 1, DEVICES), lax.rem(me + DEVICES - 1, DEVICES)
    barrier = pltpu.get_barrier_semaphore()

    @pl.loop(1, DEVICES)
    def _(j):
        pl.semaphore_signal(
            barrier, inc=1, device_id=place(lax.rem(me + j, DEVICES)), device_id_type=MESH
        )

    fetch = pltpu.make_async_copy(velocity, vel, vel_sem)
    fetch.start()

    before = jnp.where(iota((COLS, COLS), 0) < iota((COLS, COLS), 1), 1.0, 0.0).astype(BF)
    counting = jnp.concatenate([before, jnp.ones((COLS, LANES), BF)], axis=1)

    def rank_rows(r, base):
        own = owner[:, pl.ds(pl.multiple_of(r * COLS, COLS), COLS)]
        hit = jnp.broadcast_to(own, (DEVICES, COLS)) == iota((DEVICES, COLS), 0)
        p = dot(jnp.where(hit, 1.0, 0.0).astype(BF), counting)
        both = jnp.concatenate([base, base], axis=1)
        rank = jnp.sum(jnp.where(hit, p[:, :COLS] + both, 0.0), axis=0, keepdims=True)
        slot[pl.ds(r, 1), :] = own * LANES + rank.astype(I32)
        return base + p[:, COLS:]

    lax.fori_loop(0, ROWS, rank_rows, jnp.zeros((DEVICES, LANES), F32), unroll=4)

    pl.semaphore_wait(barrier, DEVICES - 1)

    last, lead = pl.ds(ROWS - 8, 8), pl.ds(0, 8)
    edge_copies = []
    for i, (target, side, part) in enumerate(((up, 0, last), (down, 1, lead))):
        for src, dst, n in (
            (positions.at[:, part, :], halo.at[side, pl.ds(0, 3)], 2 * i),
            (stiff_v.at[part, :], halo.at[side, 3], 2 * i + 1),
        ):
            edge_copies.append(
                pltpu.make_async_remote_copy(
                    src_ref=src,
                    dst_ref=dst,
                    send_sem=halo_send.at[n],
                    recv_sem=halo_recv.at[n],
                    device_id=place(target),
                    device_id_type=MESH,
                )
            )
    for copy in edge_copies:
        copy.start()
    fetch.wait()
    for k in range(3):
        high, low = split(jnp.transpose(vel[k]))
        vt[k * NODES:(k + 1) * NODES, :ELEMS] = high
        vt[k * NODES:(k + 1) * NODES, ELEMS:] = low
    ext[:, 8:8 + ROWS] = jnp.concatenate([positions[...], stiff_v[...][None]], axis=0)
    for copy in edge_copies:
        copy.wait()
    ext[:, 6:8] = halo[0, :, 6:8, :]
    ext[:, 8 + ROWS:10 + ROWS] = halo[1, :, 0:2, :]
    forces(ext, stiff_h, vals)

    acc[...] = jnp.zeros_like(acc)

    @pl.loop(0, ROWS, unroll=2)
    def _(r):
        at = pl.ds(pl.multiple_of(r * COLS, COLS), COLS)
        p = slot[pl.ds(r, 1), :]
        low_hot = one_hot(jnp.bitwise_and(p, 255), 256)
        hit = jnp.broadcast_to(lax.shift_right_logical(p, 8), (HALF, COLS)) == iota((HALF, COLS), 0)

        def picked(row):
            return jnp.where(hit, jnp.broadcast_to(row, (HALF, COLS)), 0.0).astype(BF)

        highs, lows = [], []
        for k in range(3):
            row = coords[k:k + 1, at]
            high = row.astype(BF).astype(F32)
            highs.append(picked(high))
            lows.append(picked(row - high))
        for k in range(3):
            highs.append(picked(vals[2 * k, pl.ds(r, 1), :]))
            lows.append(picked(vals[2 * k + 1, pl.ds(r, 1), :]))
        whole = picked(element[:, at].astype(F32))
        highs = jnp.concatenate(highs, axis=0)
        lows = jnp.concatenate(lows, axis=0)
        acc[:6 * HALF] += dot(highs, low_hot, NT) + dot(lows, low_hot, NT)
        acc[6 * HALF:] += dot(whole, low_hot, NT)

    for i in range(7):
        v = acc[i * HALF:(i + 1) * HALF]
        send[:, i, :] = v[:, :LANES]
        send[:, 8 + i, :] = v[:, LANES:]
    send[:, 7, :] = jnp.zeros((HALF, LANES), F32)
    send[:, 15, :] = jnp.zeros((HALF, LANES), F32)

    def block_of(t):
        return send.at[t // 2, pl.ds(pl.multiple_of(lax.rem(t, 2) * 8, 8), 8), :]

    def outward(j):
        t = lax.rem(me + j, DEVICES)
        return pltpu.make_async_remote_copy(
            src_ref=block_of(t),
            dst_ref=recv.at[me],
            send_sem=send_sem.at[j],
            recv_sem=recv_sem.at[j],
            device_id=place(t),
            device_id_type=MESH,
        )

    def homeward(j):
        t = lax.rem(me + DEVICES - j, DEVICES)
        return pltpu.make_async_remote_copy(
            src_ref=back.at[t],
            dst_ref=got.at[me],
            send_sem=back_send.at[j],
            recv_sem=back_recv.at[j],
            device_id=place(t),
            device_id_type=MESH,
        )

    @pl.loop(1, DEVICES)
    def _(j):
        outward(j).start()

    recv[me] = send[me // 2, pl.ds(pl.multiple_of(lax.rem(me, 2) * 8, 8), 8), :]
    force_acc[...] = jnp.zeros_like(force_acc)
    sampled[...] = jnp.zeros_like(sampled)
    scales = scale[...]
    lane8 = iota((8, LANES), 1)
    lane4 = iota((4, LANES), 1)

    def source(j):
        return lax.rem(me + DEVICES - j, DEVICES)

    @pl.loop(0, GROUPS)
    def _(g):
        @pl.loop(0, PER_GROUP)
        def _(i):
            @pl.when(g * PER_GROUP + i > 0)
            def _():
                outward(g * PER_GROUP + i).wait_recv()

        @pl.loop(0, PER_GROUP // 4)
        def _(q):
            b = [recv[source(g * PER_GROUP + q * 4 + i)] for i in range(4)]
            r1 = pltpu.roll(b[1], 96, 1)
            r2 = pltpu.roll(b[2], 64, 1)
            r3 = pltpu.roll(b[3], 32, 1)
            comp[q * 3] = jnp.where(lane8 < 96, b[0], r1)
            comp[q * 3 + 1] = jnp.where(lane8 < 64, r1, r2)
            comp[q * 3 + 2] = jnp.where(lane8 < 32, r2, r3)

        @pl.loop(0, PER_GROUP * CAP // CHUNK)
        def _(c):
            first = c * CHUNK_TILES
            hot = one_hot(tile_rows(comp, first, 6).astype(I32), ELEMS)
            along_r = basis(tile_rows(comp, first, 0), scales)
            along_s = basis(tile_rows(comp, first, 1), scales)
            along_t = basis(tile_rows(comp, first, 2), scales)
            stacked = jnp.concatenate([hot, hot], axis=0)
            for k in range(3):
                gk = dot(vt[k * NODES:(k + 1) * NODES, :], stacked)
                over_r = None
                for a in range(POINTS):
                    term = gk[a * 64:(a + 1) * 64] * along_r[a:a + 1]
                    over_r = term if over_r is None else over_r + term
                over_s = None
                for b in range(POINTS):
                    term = over_r[b * 8:(b + 1) * 8] * along_s[b:b + 1]
                    over_s = term if over_s is None else over_s + term
                mine = jnp.sum(over_s * along_t, axis=0, keepdims=True)
                for t in range(CHUNK_TILES):
                    sampled[first + t, k:k + 1, :] = mine[:, t * LANES:(t + 1) * LANES]
            plane = jnp.concatenate([along_s[b:b + 1] * along_t for b in range(POINTS)], axis=0)
            beside = jnp.concatenate([hot, hot], axis=1)
            for k in range(3):
                push = along_r * tile_rows(comp, first, 3 + k)
                for a in range(POINTS):
                    high, low = split(plane * push[a:a + 1])
                    at = k * NODES + a * 64
                    loads[at:at + 64, :CHUNK] = high
                    loads[at:at + 64, CHUNK:] = low
                at = k * NODES
                force_acc[at:at + NODES] += dot(loads[at:at + NODES], beside, NT)

        @pl.loop(0, PER_GROUP // 4)
        def _(q):
            s = [sampled[q * 3 + i] for i in range(3)]
            j = g * PER_GROUP + q * 4
            back[source(j)] = s[0]
            back[source(j + 1)] = pltpu.roll(jnp.where(lane4 >= 96, s[0], s[1]), 32, 1)
            back[source(j + 2)] = pltpu.roll(jnp.where(lane4 >= 64, s[1], s[2]), 64, 1)
            back[source(j + 3)] = pltpu.roll(s[2], 96, 1)

        @pl.loop(0, PER_GROUP)
        def _(i):
            @pl.when(g * PER_GROUP + i > 0)
            def _():
                homeward(g * PER_GROUP + i).start()

    for k in range(3):
        out[k] = jnp.transpose(force_acc[k * NODES:(k + 1) * NODES])
    got[me] = back[me]

    @pl.loop(1, DEVICES)
    def _(j):
        homeward(j).wait_recv()

    for k in range(3):
        both = jnp.concatenate(
            [got[pl.ds(0, HALF, stride=2), k, :], got[pl.ds(1, HALF, stride=2), k, :]], axis=1
        )
        high, low = split(both)
        table[k * HALF:(k + 1) * HALF, :COLS] = high
        table[k * HALF:(k + 1) * HALF, COLS:] = low

    @pl.loop(0, ROWS, unroll=4)
    def _(r):
        p = slot[pl.ds(r, 1), :]
        low = one_hot(jnp.bitwise_and(p, 255), 256)
        hit = jnp.broadcast_to(lax.shift_right_logical(p, 8), (HALF, COLS)) == iota((HALF, COLS), 0)
        g = dot(table[...], jnp.concatenate([low, low], axis=0))
        for k in range(3):
            mine = jnp.sum(jnp.where(hit, g[k * HALF:(k + 1) * HALF], 0.0), axis=0, keepdims=True)
            moved[k, pl.ds(r, 1), :] = positions[k, pl.ds(r, 1), :] + time_step * mine

    @pl.loop(1, DEVICES)
    def _(j):
        outward(j).wait_send()
        homeward(j).wait_send()


def local(velocity, positions, stiff_h, stiff_v, marker_owner, marker_element, marker_coords):
    markers = ROWS * COLS
    group_tiles = PER_GROUP * CAP // LANES
    vmem = pl.BlockSpec(memory_space=pltpu.VMEM)
    return pl.pallas_call(
        step,
        out_shape=(
            jax.ShapeDtypeStruct((3, ROWS, COLS), F32),
            jax.ShapeDtypeStruct((3, ELEMS, NODES), F32),
        ),
        in_specs=[vmem] * 6 + [pl.BlockSpec(memory_space=pl.ANY), vmem],
        out_specs=(vmem, vmem),
        scratch_shapes=[
            pltpu.VMEM((4, ROWS + 16, COLS), F32),
            pltpu.VMEM((2, 4, 8, COLS), F32),
            pltpu.VMEM((6, ROWS, COLS), F32),
            pltpu.VMEM((ROWS, COLS), I32),
            pltpu.VMEM((7 * HALF, COLS), F32),
            pltpu.VMEM((HALF, 16, LANES), F32),
            pltpu.VMEM((DEVICES, 8, LANES), F32),
            pltpu.VMEM((group_tiles, 8, LANES), F32),
            pltpu.VMEM((group_tiles, 4, LANES), F32),
            pltpu.VMEM((DEVICES, 4, LANES), F32),
            pltpu.VMEM((DEVICES, 4, LANES), F32),
            pltpu.VMEM((3 * HALF, 2 * COLS), BF),
            pltpu.VMEM((3, ELEMS, NODES), F32),
            pltpu.VMEM((3 * NODES, 2 * ELEMS), BF),
            pltpu.VMEM((3 * NODES, ELEMS), F32),
            pltpu.VMEM((3 * NODES, 2 * CHUNK), BF),
            pltpu.SemaphoreType.DMA,
            pltpu.SemaphoreType.DMA((4,)),
            pltpu.SemaphoreType.DMA((4,)),
            pltpu.SemaphoreType.DMA((DEVICES,)),
            pltpu.SemaphoreType.DMA((DEVICES,)),
            pltpu.SemaphoreType.DMA((DEVICES,)),
            pltpu.SemaphoreType.DMA((DEVICES,)),
        ],
        compiler_params=pltpu.CompilerParams(collective_id=0, has_side_effects=True),
        name="step",
    )(
        positions, stiff_h, stiff_v,
        marker_owner.reshape(1, markers), marker_element.reshape(1, markers), marker_coords,
        velocity, jnp.asarray(SCALE_OF),
    )


def solution(mesh):
    return jax.shard_map(
        local,
        mesh=mesh,
        in_specs=(
            P(None, ("gx", "gy"), None),
            P(None, ("gx", "gy"), None),
            P(("gx", "gy"), None),
            P(("gx", "gy"), None),
            P(("gx", "gy"), None),
            P(("gx", "gy")),
            P(None, ("gx", "gy")),
        ),
        out_specs=(P(None, ("gx", "gy"), None), P(None, ("gx", "gy"), None)),
        check_vma=False,
    )
```

time: 122 us -> 101 us (0.83)
  the two profiles are of different devices: /device:TPU:34 before, /device:TPU:1 now
where the time goes in v2:
time: 101 us
  Pallas kernels  96.3 us (95%)
  local copies, waits for them, and re-layouts  4.21 us (4%)
    pallas_call x1, Pallas kernels, local(): pl.pallas_call(step, out_shape=(jax.ShapeDtypeStruct((3, ROWS, COLS), F32...  96.3 us
    unnamed x2, local copies, waits for them, and re-layouts  4.21 us

profile of v2, /device:TPU:1, one launch (start us, length us, event | category | flops | bytes accessed | tf_op | source)
XLA Modules:
  0.0 101.1 jit_solution(16867796805083288286)
XLA Ops:
  0.6 96.3 %step.1 = (f32[3,32,256]{2,1,0:T(8,128)}, f32[3,256,512]{2,1,0:T(8,128)}) custom-call(f32[3,32,256]{2,1,0:T(8,128)} %positions.1, f32[32,256]{1,0:T(8,128)} %stiff_h.1, f32[32,256]{1,0:T(8,128)} %stiff_v.1, s32[1,8192]{1,0:T(1,128)} %bitcast.2, s32[1,8192]{1,0:T(1,128)} %bitcast.3, f32[3,8192]{1,0:T(4,128)} %coords.1, f32[3,256,512]{2,1,0:T(8,128)} %velocity.1, ...), custom_call_target="tpu_custom_call" | custom-call | tf_op jit(solution)/shard_map/step/pallas_call | solution.py:372
  96.9 1.5 %copy.12 = f32[3,32,256]{2,1,0:T(8,128)} copy(f32[3,32,256]{2,1,0:T(8,128)} %get-tuple-element.4) | data formatting | bytes 196608
  98.4 2.7 %copy.13 = f32[3,256,512]{2,1,0:T(8,128)} copy(f32[3,256,512]{2,1,0:T(8,128)} %get-tuple-element.5) | data formatting | bytes 3145728

commit v3 on v2

--- a/solution.py
+++ b/solution.py
@@ -77,11 +77,14 @@
         product = factor if product is None else product * factor
     return product
 
-MESH = pl.DeviceIdType.MESH
-
-
-def place(index):
-    return (index // 4, index % 4)
+LOGICAL = pl.DeviceIdType.LOGICAL
+
+
+def each_other(body):
+    whole = (DEVICES - 1) // 8 * 8
+    pl.loop(1, 1 + whole, unroll=8)(body)
+    for j in range(1 + whole, DEVICES):
+        body(j)
 
 
 def tile_rows(comp, first, value):
@@ -130,18 +133,18 @@
 
 
 def step(positions, stiff_h, stiff_v, owner, element, coords, velocity, scale,
-         moved, out,
-         ext, halo, vals, slot, acc, send, recv, comp, sampled, back, got, table,
-         vel, vt, force_acc, loads,
+         got_out, slot, force_acc,
+         ext, halo, vals, acc, send, recv, comp, sampled, back, got,
+         vel, vt, loads,
          vel_sem, halo_send, halo_recv, send_sem, recv_sem, back_send, back_recv):
     me = lax.axis_index("gx") * 4 + lax.axis_index("gy")
     up, down = lax.rem(me + 1, DEVICES), lax.rem(me + DEVICES - 1, DEVICES)
     barrier = pltpu.get_barrier_semaphore()
 
-    @pl.loop(1, DEVICES)
+    @each_other
     def _(j):
         pl.semaphore_signal(
-            barrier, inc=1, device_id=place(lax.rem(me + j, DEVICES)), device_id_type=MESH
+            barrier, inc=1, device_id=lax.rem(me + j, DEVICES), device_id_type=LOGICAL
         )
 
     fetch = pltpu.make_async_copy(velocity, vel, vel_sem)
@@ -176,8 +179,8 @@
                     dst_ref=dst,
                     send_sem=halo_send.at[n],
                     recv_sem=halo_recv.at[n],
-                    device_id=place(target),
-                    device_id_type=MESH,
+                    device_id=target,
+                    device_id_type=LOGICAL,
                 )
             )
     for copy in edge_copies:
@@ -229,17 +232,17 @@
     send[:, 15, :] = jnp.zeros((HALF, LANES), F32)
 
     def block_of(t):
-        return send.at[t // 2, pl.ds(pl.multiple_of(lax.rem(t, 2) * 8, 8), 8), :]
+        return send.at[lax.div(t, 2), pl.ds(pl.multiple_of(lax.rem(t, 2) * 8, 8), 8), :]
 
     def outward(j):
         t = lax.rem(me + j, DEVICES)
         return pltpu.make_async_remote_copy(
             src_ref=block_of(t),
             dst_ref=recv.at[me],
-            send_sem=send_sem.at[j],
-            recv_sem=recv_sem.at[j],
-            device_id=place(t),
-            device_id_type=MESH,
+            send_sem=send_sem,
+            recv_sem=recv_sem.at[lax.div(j, PER_GROUP)],
+            device_id=t,
+            device_id_type=LOGICAL,
         )
 
     def homeward(j):
@@ -247,13 +250,17 @@
         return pltpu.make_async_remote_copy(
             src_ref=back.at[t],
             dst_ref=got.at[me],
-            send_sem=back_send.at[j],
-            recv_sem=back_recv.at[j],
-            device_id=place(t),
-            device_id_type=MESH,
-        )
-
-    @pl.loop(1, DEVICES)
+            send_sem=back_send,
+            recv_sem=back_recv,
+            device_id=t,
+            device_id_type=LOGICAL,
+        )
+
+    def arrived(ref, count, sem):
+        part = ref.at[pl.ds(0, count)]
+        pltpu.make_async_copy(part, part, sem).wait()
+
+    @each_other
     def _(j):
         outward(j).start()
 
@@ -269,14 +276,15 @@
 
     @pl.loop(0, GROUPS)
     def _(g):
-        @pl.loop(0, PER_GROUP)
-        def _(i):
-            @pl.when(g * PER_GROUP + i > 0)
-            def _():
-                outward(g * PER_GROUP + i).wait_recv()
-
-        @pl.loop(0, PER_GROUP // 4)
-        def _(q):
+        @pl.when(g == 0)
+        def _():
+            arrived(recv, PER_GROUP - 1, recv_sem.at[g])
+
+        @pl.when(g > 0)
+        def _():
+            arrived(recv, PER_GROUP, recv_sem.at[g])
+
+        for q in range(PER_GROUP // 4):
             b = [recv[source(g * PER_GROUP + q * 4 + i)] for i in range(4)]
             r1 = pltpu.roll(b[1], 96, 1)
             r2 = pltpu.roll(b[2], 64, 1)
@@ -318,8 +326,7 @@
                 at = k * NODES
                 force_acc[at:at + NODES] += dot(loads[at:at + NODES], beside, NT)
 
-        @pl.loop(0, PER_GROUP // 4)
-        def _(q):
+        for q in range(PER_GROUP // 4):
             s = [sampled[q * 3 + i] for i in range(3)]
             j = g * PER_GROUP + q * 4
             back[source(j)] = s[0]
@@ -327,20 +334,21 @@
             back[source(j + 2)] = pltpu.roll(jnp.where(lane4 >= 64, s[1], s[2]), 64, 1)
             back[source(j + 3)] = pltpu.roll(s[2], 96, 1)
 
-        @pl.loop(0, PER_GROUP)
-        def _(i):
-            @pl.when(g * PER_GROUP + i > 0)
-            def _():
-                homeward(g * PER_GROUP + i).start()
-
-    for k in range(3):
-        out[k] = jnp.transpose(force_acc[k * NODES:(k + 1) * NODES])
+        @pl.when(g > 0)
+        def _():
+            homeward(g * PER_GROUP).start()
+
+        for i in range(1, PER_GROUP):
+            homeward(g * PER_GROUP + i).start()
+
     got[me] = back[me]
-
-    @pl.loop(1, DEVICES)
-    def _(j):
-        homeward(j).wait_recv()
-
+    arrived(got, DEVICES - 1, back_recv)
+    got_out[...] = got[...]
+    arrived(recv, DEVICES - 1, send_sem)
+    arrived(got, DEVICES - 1, back_send)
+
+
+def finish(positions, got, slot, force_acc, moved, out, table):
     for k in range(3):
         both = jnp.concatenate(
             [got[pl.ds(0, HALF, stride=2), k, :], got[pl.ds(1, HALF, stride=2), k, :]], axis=1
@@ -359,29 +367,27 @@
             mine = jnp.sum(jnp.where(hit, g[k * HALF:(k + 1) * HALF], 0.0), axis=0, keepdims=True)
             moved[k, pl.ds(r, 1), :] = positions[k, pl.ds(r, 1), :] + time_step * mine
 
-    @pl.loop(1, DEVICES)
-    def _(j):
-        outward(j).wait_send()
-        homeward(j).wait_send()
+    for k in range(3):
+        out[k] = jnp.transpose(force_acc[k * NODES:(k + 1) * NODES])
 
 
 def local(velocity, positions, stiff_h, stiff_v, marker_owner, marker_element, marker_coords):
     markers = ROWS * COLS
     group_tiles = PER_GROUP * CAP // LANES
     vmem = pl.BlockSpec(memory_space=pltpu.VMEM)
-    return pl.pallas_call(
+    got, slot, force_acc = pl.pallas_call(
         step,
         out_shape=(
-            jax.ShapeDtypeStruct((3, ROWS, COLS), F32),
-            jax.ShapeDtypeStruct((3, ELEMS, NODES), F32),
+            jax.ShapeDtypeStruct((DEVICES, 4, LANES), F32),
+            jax.ShapeDtypeStruct((ROWS, COLS), I32),
+            jax.ShapeDtypeStruct((3 * NODES, ELEMS), F32),
         ),
         in_specs=[vmem] * 6 + [pl.BlockSpec(memory_space=pl.ANY), vmem],
-        out_specs=(vmem, vmem),
+        out_specs=(vmem,) * 3,
         scratch_shapes=[
             pltpu.VMEM((4, ROWS + 16, COLS), F32),
             pltpu.VMEM((2, 4, 8, COLS), F32),
             pltpu.VMEM((6, ROWS, COLS), F32),
-            pltpu.VMEM((ROWS, COLS), I32),
             pltpu.VMEM((7 * HALF, COLS), F32),
             pltpu.VMEM((HALF, 16, LANES), F32),
             pltpu.VMEM((DEVICES, 8, LANES), F32),
@@ -389,18 +395,16 @@
             pltpu.VMEM((group_tiles, 4, LANES), F32),
             pltpu.VMEM((DEVICES, 4, LANES), F32),
             pltpu.VMEM((DEVICES, 4, LANES), F32),
-            pltpu.VMEM((3 * HALF, 2 * COLS), BF),
             pltpu.VMEM((3, ELEMS, NODES), F32),
             pltpu.VMEM((3 * NODES, 2 * ELEMS), BF),
-            pltpu.VMEM((3 * NODES, ELEMS), F32),
             pltpu.VMEM((3 * NODES, 2 * CHUNK), BF),
             pltpu.SemaphoreType.DMA,
             pltpu.SemaphoreType.DMA((4,)),
             pltpu.SemaphoreType.DMA((4,)),
-            pltpu.SemaphoreType.DMA((DEVICES,)),
-            pltpu.SemaphoreType.DMA((DEVICES,)),
-            pltpu.SemaphoreType.DMA((DEVICES,)),
-            pltpu.SemaphoreType.DMA((DEVICES,)),
+            pltpu.SemaphoreType.DMA,
+            pltpu.SemaphoreType.DMA((GROUPS,)),
+            pltpu.SemaphoreType.DMA,
+            pltpu.SemaphoreType.DMA,
         ],
         compiler_params=pltpu.CompilerParams(collective_id=0, has_side_effects=True),
         name="step",
@@ -409,6 +413,17 @@
         marker_owner.reshape(1, markers), marker_element.reshape(1, markers), marker_coords,
         velocity, jnp.asarray(SCALE_OF),
     )
+    return pl.pallas_call(
+        finish,
+        out_shape=(
+            jax.ShapeDtypeStruct((3, ROWS, COLS), F32),
+            jax.ShapeDtypeStruct((3, ELEMS, NODES), F32),
+        ),
+        in_specs=[vmem] * 4,
+        out_specs=(vmem,) * 2,
+        scratch_shapes=[pltpu.VMEM((3 * HALF, 2 * COLS), BF)],
+        name="finish",
+    )(positions, got, slot, force_acc)
 
 
 def solution(mesh):

time: 101 us -> 88.8 us (0.88)
  Pallas kernels: 96.3 us -> 88 us
  local copies, waits for them, and re-layouts: 4.21 us -> 0 us
    pallas_call x1 -> x2, Pallas kernels: 96.3 us -> 88 us  [the longest x1 81.1 us: local(): pl.pallas_call(step, out_shape=(jax.ShapeDtypeStruct((DEVICES, 4, LANES),...]
    unnamed x2 -> x0, local copies, waits for them, and re-layouts: 4.21 us -> none
where the time goes in v3:
time: 88.8 us; the launch traced here: 88.6 us
  Pallas kernels  88 us (99%)
    pallas_call x1, Pallas kernels, local(): pl.pallas_call(step, out_shape=(jax.ShapeDtypeStruct((DEVICES, 4, LANES),...  81.1 us
    pallas_call x1, Pallas kernels, local(): pl.pallas_call(finish, out_shape=(jax.ShapeDtypeStruct((3, ROWS, COLS), F...  6.88 us

profile of v3, /device:TPU:1, one launch (start us, length us, event | category | flops | bytes accessed | tf_op | source)
XLA Modules:
  0.0 88.6 jit_solution(7860225893964408680)
XLA Ops:
  0.6 81.1 %step.1 = (f32[128,4,128]{2,1,0:T(4,128)}, s32[32,256]{1,0:T(8,128)}, f32[1536,256]{1,0:T(8,128)}) custom-call(f32[3,32,256]{2,1,0:T(8,128)} %positions.3, f32[32,256]{1,0:T(8,128)} %stiff_h.1, f32[32,256]{1,0:T(8,128)} %stiff_v.1, s32[1,8192]{1,0:T(1,128)} %bitcast.2, s32[1,8192]{1,0:T(1,128)} %bitcast.3, f32[3,8192]{1,0:T(4,128)} %coords.1, ...), custom_call_target="tpu_custom_call" | custom-call | tf_op jit(solution)/shard_map/step/pallas_call | solution.py:378
  81.8 6.9 %finish.1 = (f32[3,32,256]{2,1,0:T(8,128)}, f32[3,256,512]{2,1,0:T(8,128)}) custom-call(f32[3,32,256]{2,1,0:T(8,128)} %positions.3, f32[128,4,128]{2,1,0:T(4,128)} %get-tuple-element.5.got, s32[32,256]{1,0:T(8,128)} %get-tuple-element.6.slot, f32[1536,256]{1,0:T(8,128)} %get-tuple-element.7.force_acc), custom_call_target="tpu_custom_call" | custom-call | tf_op jit(solution)/shard_map/finish/pallas_call | solution.py:416

commit v4 on v3

v4 whole, which is shorter than its diff:
```python
import math

import jax
import jax.numpy as jnp
import numpy as np
from jax import lax
from jax.experimental import pallas as pl
from jax.experimental.pallas import tpu as pltpu
from jax.sharding import PartitionSpec as P

POINTS = 8
NODES = 512
ELEMS = 256
ROWS = 32
COLS = 256
DEVICES = 128
LANES = 128
HALF = 64
TILES = 96
CHUNK = 512
CHUNK_TILES = CHUNK // LANES
CAP = 96
GROUPS = 8
PER_GROUP = DEVICES // GROUPS
LAG = 2

bend_modulus = 0.05
time_step = 0.5

BF = jnp.bfloat16
F32 = jnp.float32
I32 = jnp.int32
NN = (((1,), (0,)), ((), ()))
NT = (((1,), (1,)), ((), ()))


def dot(a, b, dims=NN):
    return lax.dot_general(a, b, dims, preferred_element_type=F32)


def iota(shape, dim):
    return lax.broadcasted_iota(I32, shape, dim)


def one_hot(row, count):
    hit = jnp.broadcast_to(row, (count, row.shape[1])) == iota((count, row.shape[1]), 0)
    return jnp.where(hit, 1.0, 0.0).astype(BF)


def split(x):
    high = x.astype(BF)
    return high, (x - high.astype(F32)).astype(BF)


def basis_tables():
    nodes = -np.cos(np.pi * np.arange(POINTS, dtype=np.float64) / (POINTS - 1))
    nodes = nodes.astype(np.float32).astype(np.float64)
    scale = np.zeros((POINTS, POINTS))
    for j in range(POINTS):
        for i in range(POINTS):
            if i != j:
                scale[j, i] = 1.0 / (nodes[i] - nodes[j])
    scale = np.broadcast_to(scale[:, :, None], (POINTS, POINTS, LANES))
    return nodes, np.ascontiguousarray(scale, np.float32)


NODE_AT, SCALE_OF = basis_tables()


def basis(row, scale):
    n = row.shape[1]
    x = jnp.broadcast_to(row, (POINTS, n))
    which = iota((POINTS, n), 0)
    product = None
    for j in range(POINTS):
        s = jnp.concatenate([scale[j]] * (n // LANES), axis=1)
        factor = jnp.where(which == j, 1.0, (x - float(NODE_AT[j])) * s)
        product = factor if product is None else product * factor
    return product

LOGICAL = pl.DeviceIdType.LOGICAL


def each_other(body):
    whole = (DEVICES - 1) // 8 * 8
    pl.loop(1, 1 + whole, unroll=8)(body)
    for j in range(1 + whole, DEVICES):
        body(j)


def tile_rows(comp, first, value):
    return jnp.concatenate([comp[first + t, value:value + 1, :] for t in range(CHUNK_TILES)], axis=1)


def chunk_of(comp, first, scales):
    hot = one_hot(tile_rows(comp, first, 3).astype(I32), ELEMS)
    return (hot, *(basis(tile_rows(comp, first, i), scales) for i in range(3)))


def sample_chunk(comp, first, scales, vt, sampled, into):
    hot, along_r, along_s, along_t = chunk_of(comp, first, scales)
    stacked = jnp.concatenate([hot, hot], axis=0)
    for k in range(3):
        gk = dot(vt[k * NODES:(k + 1) * NODES, :], stacked)
        over_r = None
        for a in range(POINTS):
            term = gk[a * 64:(a + 1) * 64] * along_r[a:a + 1]
            over_r = term if over_r is None else over_r + term
        over_s = None
        for b in range(POINTS):
            term = over_r[b * 8:(b + 1) * 8] * along_s[b:b + 1]
            over_s = term if over_s is None else over_s + term
        mine = jnp.sum(over_s * along_t, axis=0, keepdims=True)
        for t in range(CHUNK_TILES):
            sampled[into + t, k:k + 1, :] = mine[:, t * LANES:(t + 1) * LANES]


def deposit_chunk(comp, push_comp, first, scales, loads, force_acc):
    hot, along_r, along_s, along_t = chunk_of(comp, first, scales)
    plane = jnp.concatenate([along_s[b:b + 1] * along_t for b in range(POINTS)], axis=0)
    beside = jnp.concatenate([hot, hot], axis=1)
    for k in range(3):
        push = along_r * tile_rows(push_comp, first, k)
        for a in range(POINTS):
            high, low = split(plane * push[a:a + 1])
            at = k * NODES + a * 64
            loads[at:at + 64, :CHUNK] = high
            loads[at:at + 64, CHUNK:] = low
        at = k * NODES
        force_acc[at:at + NODES] += dot(loads[at:at + NODES], beside, NT)


def forces(ext, stiff_h, vals):
    def rows(k, first, count):
        return ext[k, first + 8:first + 8 + count]

    sh = stiff_h[...]
    sh_left = pltpu.roll(sh, 1, 1)
    sv = rows(3, 0, ROWS)
    sv_below = rows(3, -1, ROWS)
    for k in range(3):
        mid = rows(k, 0, ROWS)
        pull = (
            sh * (pltpu.roll(mid, COLS - 1, 1) - mid)
            + sh_left * (pltpu.roll(mid, 1, 1) - mid)
            + sv * (rows(k, 1, ROWS) - mid)
            + sv_below * (rows(k, -1, ROWS) - mid)
        )

        def lap_at(first):
            m = rows(k, first, ROWS)
            return (
                rows(k, first + 1, ROWS)
                + rows(k, first - 1, ROWS)
                + pltpu.roll(m, 1, 1)
                + pltpu.roll(m, COLS - 1, 1)
                - 4.0 * m
            )

        lap = lap_at(0)
        bend = (
            lap_at(1)
            + lap_at(-1)
            + pltpu.roll(lap, 1, 1)
            + pltpu.roll(lap, COLS - 1, 1)
            - 4.0 * lap
        )
        force = pull - bend_modulus * bend
        high = force.astype(BF).astype(F32)
        vals[2 * k] = high
        vals[2 * k + 1] = force - high


def step(positions_in, stiff_h_in, stiff_v_in, owner_in, element_in, coords_in, velocity, scale,
         got_out, slot, force_out,
         positions, stiff_h, stiff_v, owner, element, coords, force_acc,
         ext, halo, vals, acc, send, recv, push_send, push_recv, comp, push_comp, sampled, back, got,
         vel, vt, loads,
         in_sems, out_sem, vel_sem, halo_send, halo_recv, send_sem, recv_sem, push_send_sem, push_recv_sem,
         back_send, back_recv):
    me = lax.axis_index("gx") * 4 + lax.axis_index("gy")
    up, down = lax.rem(me + 1, DEVICES), lax.rem(me + DEVICES - 1, DEVICES)
    barrier = pltpu.get_barrier_semaphore()

    ins = [
        pltpu.make_async_copy(src, dst, in_sems.at[i])
        for i, (src, dst) in enumerate((
            (owner_in, owner), (positions_in, positions), (stiff_v_in, stiff_v),
            (coords_in, coords), (element_in, element), (stiff_h_in, stiff_h),
        ))
    ]
    for copy in ins:
        copy.start()
    fetch = pltpu.make_async_copy(velocity, vel, vel_sem)
    fetch.start()

    @each_other
    def _(j):
        pl.semaphore_signal(
            barrier, inc=1, device_id=lax.rem(me + j, DEVICES), device_id_type=LOGICAL
        )

    ins[0].wait()

    before = jnp.where(iota((COLS, COLS), 0) < iota((COLS, COLS), 1), 1.0, 0.0).astype(BF)
    counting = jnp.concatenate([before, jnp.ones((COLS, LANES), BF)], axis=1)

    def rank_rows(r, base):
        own = owner[:, pl.ds(pl.multiple_of(r * COLS, COLS), COLS)]
        hit = jnp.broadcast_to(own, (DEVICES, COLS)) == iota((DEVICES, COLS), 0)
        p = dot(jnp.where(hit, 1.0, 0.0).astype(BF), counting)
        both = jnp.concatenate([base, base], axis=1)
        rank = jnp.sum(jnp.where(hit, p[:, :COLS] + both, 0.0), axis=0, keepdims=True)
        slot[pl.ds(r, 1), :] = own * LANES + rank.astype(I32)
        return base + p[:, COLS:]

    lax.fori_loop(0, ROWS, rank_rows, jnp.zeros((DEVICES, LANES), F32), unroll=4)

    fetch.wait()
    for k in range(3):
        high, low = split(jnp.transpose(vel[k]))
        vt[k * NODES:(k + 1) * NODES, :ELEMS] = high
        vt[k * NODES:(k + 1) * NODES, ELEMS:] = low

    for copy in ins[1:]:
        copy.wait()
    pl.semaphore_wait(barrier, DEVICES - 1)

    last, lead = pl.ds(ROWS - 8, 8), pl.ds(0, 8)
    edge_copies = []
    for i, (target, side, part) in enumerate(((up, 0, last), (down, 1, lead))):
        for src, dst, n in (
            (positions.at[:, part, :], halo.at[side, pl.ds(0, 3)], 2 * i),
            (stiff_v.at[part, :], halo.at[side, 3], 2 * i + 1),
        ):
            edge_copies.append(
                pltpu.make_async_remote_copy(
                    src_ref=src,
                    dst_ref=dst,
                    send_sem=halo_send.at[n],
                    recv_sem=halo_recv.at[n],
                    device_id=target,
                    device_id_type=LOGICAL,
                )
            )
    for copy in edge_copies:
        copy.start()

    def spread(values, lows, whole, to):
        count = len(lows)
        total = 2 * count + whole
        acc[:total * HALF] = jnp.zeros((total * HALF, COLS), F32)

        @pl.loop(0, ROWS // 2, unroll=4)
        def _(h):
            r = h * 2
            p = jnp.concatenate([slot[pl.ds(r, 1), :], slot[pl.ds(r + 1, 1), :]], axis=1)
            low_hot = one_hot(jnp.bitwise_and(p, 255), 256)
            shape = (HALF, 2 * COLS)
            hit = jnp.broadcast_to(lax.shift_right_logical(p, 8), shape) == iota(shape, 0)
            picked = [
                jnp.where(hit, jnp.broadcast_to(row, shape), 0.0).astype(BF) for row in values(h)
            ]
            acc[:total * HALF] += dot(jnp.concatenate(picked, axis=0), low_hot, NT)

        for i in range(count + whole):
            v = acc[i * HALF:(i + 1) * HALF]
            if i < count:
                n = count + whole + i
                v = v + acc[n * HALF:(n + 1) * HALF]
            to[pl.ds(0, HALF, stride=2), i, :] = v[:, :LANES]
            to[pl.ds(1, HALF, stride=2), i, :] = v[:, LANES:]

    def place_rows(h):
        at = pl.ds(pl.multiple_of(h * 2 * COLS, 2 * COLS), 2 * COLS)
        rows = [coords[k:k + 1, at] for k in range(3)]
        highs = [row.astype(BF).astype(F32) for row in rows]
        return highs + [element[:, at].astype(F32)] + [r - h for r, h in zip(rows, highs)]

    def push_rows(h):
        def both(i):
            return jnp.concatenate([vals[i, pl.ds(h * 2, 1), :], vals[i, pl.ds(h * 2 + 1, 1), :]], axis=1)

        return [both(2 * k) for k in range(3)] + [both(2 * k + 1) for k in range(3)]

    spread(place_rows, (0, 1, 2), 1, send)

    def outward(j, src, dst, sent, landed):
        t = lax.rem(me + j, DEVICES)
        return pltpu.make_async_remote_copy(
            src_ref=src.at[t],
            dst_ref=dst.at[me],
            send_sem=sent,
            recv_sem=landed.at[lax.div(j, PER_GROUP)],
            device_id=t,
            device_id_type=LOGICAL,
        )

    def source(j):
        return lax.rem(me + DEVICES - j, DEVICES)

    def homeward(j):
        t = source(j)
        return pltpu.make_async_remote_copy(
            src_ref=back.at[t],
            dst_ref=got.at[me],
            send_sem=back_send,
            recv_sem=back_recv,
            device_id=t,
            device_id_type=LOGICAL,
        )

    def arrived(ref, count, sem):
        part = ref.at[pl.ds(0, count)]
        pltpu.make_async_copy(part, part, sem).wait()

    @each_other
    def _(j):
        outward(j, send, recv, send_sem, recv_sem).start()

    recv[me] = send[me]

    ext[:, 8:8 + ROWS] = jnp.concatenate([positions[...], stiff_v[...][None]], axis=0)
    for copy in edge_copies:
        copy.wait()
    ext[:, 6:8] = halo[0, :, 6:8, :]
    ext[:, 8 + ROWS:10 + ROWS] = halo[1, :, 0:2, :]
    forces(ext, stiff_h, vals)
    push_send[:, 3, :] = jnp.zeros((DEVICES, LANES), F32)
    spread(push_rows, (0, 1, 2), 0, push_send)

    @each_other
    def _(j):
        outward(j, push_send, push_recv, push_send_sem, push_recv_sem).start()

    push_recv[me] = push_send[me]

    force_acc[...] = jnp.zeros_like(force_acc)
    sampled[...] = jnp.zeros_like(sampled)
    scales = scale[...]
    lane4 = iota((4, LANES), 1)
    tiles = PER_GROUP * CAP // LANES
    chunks = PER_GROUP * CAP // CHUNK

    def pack(g, blocks, packed):
        for q in range(PER_GROUP // 4):
            b = [blocks[source(g * PER_GROUP + q * 4 + i)] for i in range(4)]
            r1 = pltpu.roll(b[1], 96, 1)
            r2 = pltpu.roll(b[2], 64, 1)
            r3 = pltpu.roll(b[3], 32, 1)
            at = g * tiles + q * 3
            packed[at] = jnp.where(lane4 < 96, b[0], r1)
            packed[at + 1] = jnp.where(lane4 < 64, r1, r2)
            packed[at + 2] = jnp.where(lane4 < 32, r2, r3)

    def send_back(g, own):
        for q in range(PER_GROUP // 4):
            s = [sampled[q * 3 + i] for i in range(3)]
            j = g * PER_GROUP + q * 4
            back[source(j)] = s[0]
            back[source(j + 1)] = pltpu.roll(jnp.where(lane4 >= 96, s[0], s[1]), 32, 1)
            back[source(j + 2)] = pltpu.roll(jnp.where(lane4 >= 64, s[1], s[2]), 64, 1)
            back[source(j + 3)] = pltpu.roll(s[2], 96, 1)
        for i in range(1 if own else 0, PER_GROUP):
            homeward(g * PER_GROUP + i).start()

    def sample_group(g):
        @pl.loop(0, chunks)
        def _(c):
            at = c * CHUNK_TILES
            sample_chunk(comp, g * tiles + at, scales, vt, sampled, at)

    arrived(recv, PER_GROUP - 1, recv_sem.at[0])
    pack(0, recv, comp)
    sample_group(0)
    send_back(0, True)
    got[me] = back[me]

    @pl.loop(1, LAG)
    def _(g):
        arrived(recv, PER_GROUP, recv_sem.at[g])
        pack(g, recv, comp)
        sample_group(g)
        send_back(g, False)

    arrived(push_recv, PER_GROUP - 1, push_recv_sem.at[0])
    pack(0, push_recv, push_comp)

    @pl.loop(LAG, GROUPS)
    def _(g):
        arrived(recv, PER_GROUP, recv_sem.at[g])
        pack(g, recv, comp)

        @pl.loop(0, chunks)
        def _(c):
            at = c * CHUNK_TILES
            sample_chunk(comp, g * tiles + at, scales, vt, sampled, at)
            deposit_chunk(comp, push_comp, (g - LAG) * tiles + at, scales, loads, force_acc)

        send_back(g, False)
        arrived(push_recv, PER_GROUP, push_recv_sem.at[g - LAG + 1])
        pack(g - LAG + 1, push_recv, push_comp)

    @pl.loop(GROUPS - LAG, GROUPS)
    def _(g):
        @pl.loop(0, chunks)
        def _(c):
            deposit_chunk(comp, push_comp, g * tiles + c * CHUNK_TILES, scales, loads, force_acc)

        @pl.when(g < GROUPS - 1)
        def _():
            arrived(push_recv, PER_GROUP, push_recv_sem.at[g + 1])
            pack(g + 1, push_recv, push_comp)

    flush = pltpu.make_async_copy(force_acc, force_out, out_sem)
    flush.start()
    arrived(got, DEVICES - 1, back_recv)
    got_out[...] = got[...]
    arrived(recv, DEVICES - 1, send_sem)
    arrived(recv, DEVICES - 1, push_send_sem)
    arrived(got, DEVICES - 1, back_send)
    flush.wait()


def finish(positions, got, slot, force_in, moved, out, table, force_acc, turned, in_sem, out_sem):
    ins, outs = [], []
    for k in range(3):
        part = pl.ds(k * NODES, NODES)
        ins.append(pltpu.make_async_copy(force_in.at[part], force_acc.at[part], in_sem.at[k]))
        outs.append(pltpu.make_async_copy(turned.at[k], out.at[k], out_sem.at[k]))
    for copy in ins:
        copy.start()
    for k in range(3):
        both = jnp.concatenate(
            [got[pl.ds(0, HALF, stride=2), k, :], got[pl.ds(1, HALF, stride=2), k, :]], axis=1
        )
        high, low = split(both)
        table[k * HALF:(k + 1) * HALF, :COLS] = high
        table[k * HALF:(k + 1) * HALF, COLS:] = low

    @pl.loop(0, ROWS, unroll=4)
    def _(r):
        p = slot[pl.ds(r, 1), :]
        low = one_hot(jnp.bitwise_and(p, 255), 256)
        hit = jnp.broadcast_to(lax.shift_right_logical(p, 8), (HALF, COLS)) == iota((HALF, COLS), 0)
        g = dot(table[...], jnp.concatenate([low, low], axis=0))
        for k in range(3):
            mine = jnp.sum(jnp.where(hit, g[k * HALF:(k + 1) * HALF], 0.0), axis=0, keepdims=True)
            moved[k, pl.ds(r, 1), :] = positions[k, pl.ds(r, 1), :] + time_step * mine

    for k in range(3):
        ins[k].wait()
        turned[k] = jnp.transpose(force_acc[k * NODES:(k + 1) * NODES])
        outs[k].start()
    for copy in outs:
        copy.wait()


def local(velocity, positions, stiff_h, stiff_v, marker_owner, marker_element, marker_coords):
    markers = ROWS * COLS
    group_tiles = PER_GROUP * CAP // LANES
    vmem = pl.BlockSpec(memory_space=pltpu.VMEM)
    got, slot, force_acc = pl.pallas_call(
        step,
        out_shape=(
            jax.ShapeDtypeStruct((DEVICES, 4, LANES), F32),
            jax.ShapeDtypeStruct((ROWS, COLS), I32),
            jax.ShapeDtypeStruct((3 * NODES, ELEMS), F32),
        ),
        in_specs=[pl.BlockSpec(memory_space=pl.ANY)] * 7 + [vmem],
        out_specs=(vmem, vmem, pl.BlockSpec(memory_space=pl.ANY)),
        scratch_shapes=[
            pltpu.VMEM((3, ROWS, COLS), F32),
            pltpu.VMEM((ROWS, COLS), F32),
            pltpu.VMEM((ROWS, COLS), F32),
            pltpu.VMEM((1, markers), I32),
            pltpu.VMEM((1, markers), I32),
            pltpu.VMEM((3, markers), F32),
            pltpu.VMEM((3 * NODES, ELEMS), F32),
            pltpu.VMEM((4, ROWS + 16, COLS), F32),
            pltpu.VMEM((2, 4, 8, COLS), F32),
            pltpu.VMEM((6, ROWS, COLS), F32),
            pltpu.VMEM((7 * HALF, COLS), F32),
            pltpu.VMEM((DEVICES, 4, LANES), F32),
            pltpu.VMEM((DEVICES, 4, LANES), F32),
            pltpu.VMEM((DEVICES, 4, LANES), F32),
            pltpu.VMEM((DEVICES, 4, LANES), F32),
            pltpu.VMEM((TILES, 4, LANES), F32),
            pltpu.VMEM((TILES, 4, LANES), F32),
            pltpu.VMEM((group_tiles, 4, LANES), F32),
            pltpu.VMEM((DEVICES, 4, LANES), F32),
            pltpu.VMEM((DEVICES, 4, LANES), F32),
            pltpu.VMEM((3, ELEMS, NODES), F32),
            pltpu.VMEM((3 * NODES, 2 * ELEMS), BF),
            pltpu.VMEM((3 * NODES, 2 * CHUNK), BF),
            pltpu.SemaphoreType.DMA((6,)),
            pltpu.SemaphoreType.DMA,
            pltpu.SemaphoreType.DMA,
            pltpu.SemaphoreType.DMA((4,)),
            pltpu.SemaphoreType.DMA((4,)),
            pltpu.SemaphoreType.DMA,
            pltpu.SemaphoreType.DMA((GROUPS,)),
            pltpu.SemaphoreType.DMA,
            pltpu.SemaphoreType.DMA((GROUPS,)),
            pltpu.SemaphoreType.DMA,
            pltpu.SemaphoreType.DMA,
        ],
        compiler_params=pltpu.CompilerParams(collective_id=0, has_side_effects=True),
        name="step",
    )(
        positions, stiff_h, stiff_v,
        marker_owner.reshape(1, markers), marker_element.reshape(1, markers), marker_coords,
        velocity, jnp.asarray(SCALE_OF),
    )
    return pl.pallas_call(
        finish,
        out_shape=(
            jax.ShapeDtypeStruct((3, ROWS, COLS), F32),
            jax.ShapeDtypeStruct((3, ELEMS, NODES), F32),
        ),
        in_specs=[vmem] * 3 + [pl.BlockSpec(memory_space=pl.ANY)],
        out_specs=(vmem, pl.BlockSpec(memory_space=pl.ANY)),
        scratch_shapes=[
            pltpu.VMEM((3 * HALF, 2 * COLS), BF),
            pltpu.VMEM((3 * NODES, ELEMS), F32),
            pltpu.VMEM((3, ELEMS, NODES), F32),
            pltpu.SemaphoreType.DMA((3,)),
            pltpu.SemaphoreType.DMA((3,)),
        ],
        name="finish",
    )(positions, got, slot, force_acc)


def solution(mesh):
    return jax.shard_map(
        local,
        mesh=mesh,
        in_specs=(
            P(None, ("gx", "gy"), None),
            P(None, ("gx", "gy"), None),
            P(("gx", "gy"), None),
            P(("gx", "gy"), None),
            P(("gx", "gy"), None),
            P(("gx", "gy")),
            P(None, ("gx", "gy")),
        ),
        out_specs=(P(None, ("gx", "gy"), None), P(None, ("gx", "gy"), None)),
        check_vma=False,
    )
```

time: 88.8 us -> 78.3 us (0.88)
  Pallas kernels: 88 us -> 77.4 us
    pallas_call x1, Pallas kernels: 81.1 us -> 70.7 us  [local(): pl.pallas_call(step, out_shape=(jax.ShapeDtypeStruct((DEVICES, 4, LANES),...]
where the time goes in v4:
time: 78.3 us; the launch traced here: 78.1 us
  Pallas kernels  77.4 us (99%)
    pallas_call x1, Pallas kernels, local(): pl.pallas_call(step, out_shape=(jax.ShapeDtypeStruct((DEVICES, 4, LANES),...  70.7 us
    pallas_call x1, Pallas kernels, local(): pl.pallas_call(finish, out_shape=(jax.ShapeDtypeStruct((3, ROWS, COLS), F...  6.77 us

profile of v4, /device:TPU:1, one launch (start us, length us, event | category | flops | bytes accessed | tf_op | source)
XLA Modules:
  0.0 78.1 jit_solution(17528339127861119316)
XLA Ops:
  0.6 70.7 %step.1 = (f32[128,4,128]{2,1,0:T(4,128)}, s32[32,256]{1,0:T(8,128)}, f32[1536,256]{1,0:T(8,128)}) custom-call(f32[3,32,256]{2,1,0:T(8,128)} %positions.1, f32[32,256]{1,0:T(8,128)} %stiff_h_in.1, f32[32,256]{1,0:T(8,128)} %stiff_v_in.1, s32[1,8192]{1,0:T(1,128)} %bitcast.2, s32[1,8192]{1,0:T(1,128)} %bitcast.3, f32[3,8192]{1,0:T(4,128)} %coords_in.1, ...), custom_call_target="tpu_custom_call" | custom-call | tf_op jit(solution)/shard_map/step/pallas_call | solution.py:463
  71.3 6.8 %finish.1 = (f32[3,32,256]{2,1,0:T(8,128)}, f32[3,256,512]{2,1,0:T(8,128)}) custom-call(f32[3,32,256]{2,1,0:T(8,128)} %positions.1, f32[128,4,128]{2,1,0:T(4,128)} %get-tuple-element.5.got, s32[32,256]{1,0:T(8,128)} %get-tuple-element.6.slot, f32[1536,256]{1,0:T(8,128)} %get-tuple-element.7.force_in), custom_call_target="tpu_custom_call" | custom-call | tf_op jit(solution)/shard_map/finish/pallas_call | solution.py:515

commit v5 on v4

--- a/solution.py
+++ b/solution.py
@@ -23,6 +23,7 @@
 GROUPS = 8
 PER_GROUP = DEVICES // GROUPS
 LAG = 2
+EARLY = 8
 
 bend_modulus = 0.05
 time_step = 0.5
@@ -214,7 +215,7 @@
         slot[pl.ds(r, 1), :] = own * LANES + rank.astype(I32)
         return base + p[:, COLS:]
 
-    lax.fori_loop(0, ROWS, rank_rows, jnp.zeros((DEVICES, LANES), F32), unroll=4)
+    lax.fori_loop(0, ROWS, rank_rows, jnp.zeros((DEVICES, LANES), F32), unroll=8)
 
     fetch.wait()
     for k in range(3):
@@ -251,7 +252,7 @@
         total = 2 * count + whole
         acc[:total * HALF] = jnp.zeros((total * HALF, COLS), F32)
 
-        @pl.loop(0, ROWS // 2, unroll=4)
+        @pl.loop(0, ROWS // 2, unroll=8)
         def _(h):
             r = h * 2
             p = jnp.concatenate([slot[pl.ds(r, 1), :], slot[pl.ds(r + 1, 1), :]], axis=1)
@@ -438,8 +439,7 @@
         table[k * HALF:(k + 1) * HALF, :COLS] = high
         table[k * HALF:(k + 1) * HALF, COLS:] = low
 
-    @pl.loop(0, ROWS, unroll=4)
-    def _(r):
+    def one_row(r):
         p = slot[pl.ds(r, 1), :]
         low = one_hot(jnp.bitwise_and(p, 255), 256)
         hit = jnp.broadcast_to(lax.shift_right_logical(p, 8), (HALF, COLS)) == iota((HALF, COLS), 0)
@@ -448,10 +448,12 @@
             mine = jnp.sum(jnp.where(hit, g[k * HALF:(k + 1) * HALF], 0.0), axis=0, keepdims=True)
             moved[k, pl.ds(r, 1), :] = positions[k, pl.ds(r, 1), :] + time_step * mine
 
+    pl.loop(0, EARLY, unroll=4)(one_row)
     for k in range(3):
         ins[k].wait()
         turned[k] = jnp.transpose(force_acc[k * NODES:(k + 1) * NODES])
         outs[k].start()
+    pl.loop(EARLY, ROWS, unroll=4)(one_row)
     for copy in outs:
         copy.wait()
 

time: 78.3 us -> 76.7 us (0.980)
  Pallas kernels: 77.4 us -> 75.8 us
    pallas_call x1, Pallas kernels: 70.7 us -> 69.8 us  [local(): pl.pallas_call(step, out_shape=(jax.ShapeDtypeStruct((DEVICES, 4, LANES),...]
where the time goes in v5:
time: 76.7 us; the launch traced here: 76.5 us
  Pallas kernels  75.8 us (99%)
    pallas_call x1, Pallas kernels, local(): pl.pallas_call(step, out_shape=(jax.ShapeDtypeStruct((DEVICES, 4, LANES),...  69.8 us
    pallas_call x1, Pallas kernels, local(): pl.pallas_call(finish, out_shape=(jax.ShapeDtypeStruct((3, ROWS, COLS), F...  6.01 us

profile of v5, /device:TPU:1, one launch (start us, length us, event | category | flops | bytes accessed | tf_op | source)
XLA Modules:
  0.0 76.5 jit_solution(15090444684987277598)
XLA Ops:
  0.6 69.8 %step.1 = (f32[128,4,128]{2,1,0:T(4,128)}, s32[32,256]{1,0:T(8,128)}, f32[1536,256]{1,0:T(8,128)}) custom-call(f32[3,32,256]{2,1,0:T(8,128)} %positions.1, f32[32,256]{1,0:T(8,128)} %stiff_h_in.1, f32[32,256]{1,0:T(8,128)} %stiff_v_in.1, s32[1,8192]{1,0:T(1,128)} %bitcast.2, s32[1,8192]{1,0:T(1,128)} %bitcast.3, f32[3,8192]{1,0:T(4,128)} %coords_in.1, ...), custom_call_target="tpu_custom_call" | custom-call | tf_op jit(solution)/shard_map/step/pallas_call | solution.py:465
  70.4 6.0 %finish.1 = (f32[3,32,256]{2,1,0:T(8,128)}, f32[3,256,512]{2,1,0:T(8,128)}) custom-call(f32[3,32,256]{2,1,0:T(8,128)} %positions.1, f32[128,4,128]{2,1,0:T(4,128)} %get-tuple-element.5.got, s32[32,256]{1,0:T(8,128)} %get-tuple-element.6.slot, f32[1536,256]{1,0:T(8,128)} %get-tuple-element.7.force_in), custom_call_target="tpu_custom_call" | custom-call | tf_op jit(solution)/shard_map/finish/pallas_call | solution.py:517

commit v6 on v5

--- a/solution.py
+++ b/solution.py
@@ -448,12 +448,12 @@
             mine = jnp.sum(jnp.where(hit, g[k * HALF:(k + 1) * HALF], 0.0), axis=0, keepdims=True)
             moved[k, pl.ds(r, 1), :] = positions[k, pl.ds(r, 1), :] + time_step * mine
 
-    pl.loop(0, EARLY, unroll=4)(one_row)
+    pl.loop(0, EARLY, unroll=8)(one_row)
     for k in range(3):
         ins[k].wait()
         turned[k] = jnp.transpose(force_acc[k * NODES:(k + 1) * NODES])
         outs[k].start()
-    pl.loop(EARLY, ROWS, unroll=4)(one_row)
+    pl.loop(EARLY, ROWS, unroll=8)(one_row)
     for copy in outs:
         copy.wait()
 

time: 76.7 us -> 76.4 us (level)
  no operation moved by 1% of the time
where the time goes in v6:
time: 76.4 us; the launch traced here: 76.2 us
  Pallas kernels  75.5 us (99%)
    pallas_call x1, Pallas kernels, local(): pl.pallas_call(step, out_shape=(jax.ShapeDtypeStruct((DEVICES, 4, LANES),...  69.8 us
    pallas_call x1, Pallas kernels, local(): pl.pallas_call(finish, out_shape=(jax.ShapeDtypeStruct((3, ROWS, COLS), F...  5.7 us

profile of v6, /device:TPU:1, one launch (start us, length us, event | category | flops | bytes accessed | tf_op | source)
XLA Modules:
  0.0 76.2 jit_solution(16411259544811576572)
XLA Ops:
  0.6 69.8 %step.1 = (f32[128,4,128]{2,1,0:T(4,128)}, s32[32,256]{1,0:T(8,128)}, f32[1536,256]{1,0:T(8,128)}) custom-call(f32[3,32,256]{2,1,0:T(8,128)} %positions.1, f32[32,256]{1,0:T(8,128)} %stiff_h_in.1, f32[32,256]{1,0:T(8,128)} %stiff_v_in.1, s32[1,8192]{1,0:T(1,128)} %bitcast.2, s32[1,8192]{1,0:T(1,128)} %bitcast.3, f32[3,8192]{1,0:T(4,128)} %coords_in.1, ...), custom_call_target="tpu_custom_call" | custom-call | tf_op jit(solution)/shard_map/step/pallas_call | solution.py:465
  70.4 5.7 %finish.1 = (f32[3,32,256]{2,1,0:T(8,128)}, f32[3,256,512]{2,1,0:T(8,128)}) custom-call(f32[3,32,256]{2,1,0:T(8,128)} %positions.1, f32[128,4,128]{2,1,0:T(4,128)} %get-tuple-element.5.got, s32[32,256]{1,0:T(8,128)} %get-tuple-element.6.slot, f32[1536,256]{1,0:T(8,128)} %get-tuple-element.7.force_in), custom_call_target="tpu_custom_call" | custom-call | tf_op jit(solution)/shard_map/finish/pallas_call | solution.py:517
